TPU v7x, 32 devices: a whole 2x2x4 slice. The times are simulated.
32 devices in a mesh: dp: 8 (over z, y), tensor: 4 (over x, core).
Axes of the slice: x: 2, y: 2, z: 4, core: 2. Of those that a mesh axis runs over, the one named last changes fastest.
Arguments:
- tokens: bfloat16 [16384, 768], P(('dp', 'tensor')), may hold values from -6 to 6
- lengths: int32 [8], P('dp'), may hold values from 512 to 2048, as said below
- qkv_weight: bfloat16 [3, 768, 768], P(None, 'dp', 'tensor'), may hold values from -0.21875 to 0.21875
- qv_bias: float32 [2, 768], replicated, may hold values from -0.75 to 0.75
- out_weight: bfloat16 [768, 768], P('tensor', 'dp'), may hold values from -6 to 6
- out_bias: float32 [768], replicated, may hold values from -4 to 4
- first_gain: float32 [768], replicated, may hold values from 0.5 to 1.5
- first_shift: float32 [768], replicated, may hold values from -4 to 4
- up_weight: bfloat16 [768, 3072], P('dp', 'tensor'), may hold values from -0.21875 to 0.21875
- up_bias: float32 [3072], replicated, may hold values from -6 to 6
- down_weight: bfloat16 [3072, 768], P('tensor', 'dp'), may hold values from -0.109375 to 0.109375
- down_bias: float32 [768], replicated, may hold values from -4 to 4
- second_gain: float32 [768], replicated, may hold values from 0.5 to 1.5
- second_shift: float32 [768], replicated, may hold values from -4 to 4
- cotangent: bfloat16 [16384, 768], P(('dp', 'tensor')), may hold values from -6 to 6
Outputs:
- layer_out: bfloat16 [16384, 768], P(('dp', 'tensor'))
- grad_tokens: float32 [16384, 768], P(('dp', 'tensor'))
- grad_qkv_weight: float32 [3, 768, 768], P(None, 'dp', 'tensor')
- grad_qv_bias: float32 [2, 768], P(None, ('dp', 'tensor'))
- grad_out_weight: float32 [768, 768], P('tensor', 'dp')
- grad_out_bias: float32 [768], P(('dp', 'tensor'))
- grad_first_gain: float32 [768], P(('dp', 'tensor'))
- grad_first_shift: float32 [768], P(('dp', 'tensor'))
- grad_up_weight: float32 [768, 3072], P('dp', 'tensor')
- grad_up_bias: float32 [3072], P(('dp', 'tensor'))
- grad_down_weight: float32 [3072, 768], P('tensor', 'dp')
- grad_down_bias: float32 [768], P(('dp', 'tensor'))
- grad_second_gain: float32 [768], P(('dp', 'tensor'))
- grad_second_shift: float32 [768], P(('dp', 'tensor'))
Inputs may be any that keep to these rules, and one draw needn't show every extreme that they name: `lengths`: each slot's valid tokens come first; some slot is full, with 2048 valid tokens.
All inputs are finite; a program needn't handle non-finite values.
Results may differ from a plain program's by a relative error of at most 0.02.
Values may be sent and summed in bfloat16 or wider, within the bound.
A program may use at most 128 MiB of HBM per device.

v0:
```python
import math

import jax
import jax.numpy as jnp
from jax import lax
from jax.sharding import PartitionSpec as P

D = 768
HEAD = 64
FF = 3072


NEGATIVE = -1e30
EPSILON = 1e-05


def gelu_tanh(values):
    bracket = 0.7978845608028654 * (values + 0.044715 * values * values * values)
    return 0.5 * values * (1.0 + jnp.tanh(bracket))


def norm_rows(hidden, scaling, offset):
    centered = hidden - jnp.mean(hidden, axis=-1, keepdims=True)
    inverse = lax.rsqrt(jnp.mean(centered * centered, axis=-1, keepdims=True) + EPSILON)
    normed = centered * inverse
    return (normed * scaling + offset, normed, inverse)


def norm_back(upstream, normed, inverse, scaling):
    scaled = upstream * scaling
    bracket = (
        scaled
        - jnp.mean(scaled, axis=-1, keepdims=True)
        - normed * jnp.mean(scaled * normed, axis=-1, keepdims=True)
    )
    return (inverse * bracket, jnp.sum(upstream * normed, axis=0), jnp.sum(upstream, axis=0))


def per_device(
    tokens,
    lengths,
    qkv_weight,
    qv_bias,
    out_weight,
    out_bias,
    first_gain,
    first_shift,
    up_weight,
    up_bias,
    down_weight,
    down_bias,
    second_gain,
    second_shift,
    cotangent,
):
    local_rows = tokens.shape[0]
    piece = lax.axis_index("tensor")
    head_cols = qkv_weight.shape[2]
    unit_cols = up_weight.shape[1]
    head_count = head_cols // HEAD
    scale = 1.0 / math.sqrt(HEAD)
    length = lengths[0]
    qkv_full, out_full, up_full, down_full = (
        lax.all_gather(qkv_weight, "dp", axis=1, tiled=True),
        lax.all_gather(out_weight, "dp", axis=1, tiled=True),
        lax.all_gather(up_weight, "dp", axis=0, tiled=True),
        lax.all_gather(down_weight, "dp", axis=1, tiled=True),
    )
    seq_tokens = lax.all_gather(tokens, "tensor", axis=0, tiled=True)
    total_rows = seq_tokens.shape[0]
    block = min(512, total_rows)
    blocks = total_rows // block
    key_valid = jnp.arange(total_rows, dtype=jnp.int32) < length
    row_start = piece * local_rows
    row_valid = row_start + jnp.arange(local_rows, dtype=jnp.int32) < length
    head_start = piece * head_cols
    unit_start = piece * unit_cols
    bias_cols = lax.dynamic_slice_in_dim(qv_bias, head_start, head_cols, 1)
    projected = jnp.einsum("sd,jdc->jsc", seq_tokens, qkv_full, preferred_element_type=jnp.float32)
    queries = (projected[0] + bias_cols[0]).astype(jnp.bfloat16)
    key_rows = projected[1].astype(jnp.bfloat16)
    value_rows = (projected[2] + bias_cols[1]).astype(jnp.bfloat16)
    query_heads = queries.reshape(total_rows, head_count, HEAD)
    key_heads = key_rows.reshape(total_rows, head_count, HEAD)
    value_heads = value_rows.reshape(total_rows, head_count, HEAD)
    query_blocks = query_heads.reshape(blocks, block, head_count, HEAD)

    def attend_block(query_block):
        scores = (
            jnp.einsum("qhd,khd->hqk", query_block, key_heads, preferred_element_type=jnp.float32)
            * scale
        )
        scores = jnp.where(key_valid[None, None, :], scores, NEGATIVE)
        top_score = jnp.max(scores, axis=-1, keepdims=True)
        expo = jnp.exp(scores - top_score)
        row_total = jnp.sum(expo, axis=-1, keepdims=True)
        probs = (expo / row_total).astype(jnp.bfloat16)
        context = jnp.einsum("hqk,khd->qhd", probs, value_heads, preferred_element_type=jnp.float32)
        return (context.astype(jnp.bfloat16), (top_score + jnp.log(row_total))[..., 0])

    context_blocks, log_totals = lax.map(attend_block, query_blocks)
    mixed = context_blocks.reshape(total_rows, head_cols)
    out_part = jnp.dot(mixed, out_full, preferred_element_type=jnp.float32)
    attn_local = lax.psum_scatter(
        out_part.astype(jnp.bfloat16), "tensor", scatter_dimension=0, tiled=True
    ).astype(jnp.float32)
    first_out, first_normed, first_inverse = norm_rows(
        tokens.astype(jnp.float32) + (attn_local + out_bias), first_gain, first_shift
    )
    first_low = first_out.astype(jnp.bfloat16)
    seq_first = lax.all_gather(first_low, "tensor", axis=0, tiled=True)
    up_cols = lax.dynamic_slice_in_dim(up_bias, unit_start, unit_cols, 0)
    pre_act = jnp.dot(seq_first, up_full, preferred_element_type=jnp.float32) + up_cols
    activated = gelu_tanh(pre_act).astype(jnp.bfloat16)
    ffn_local = lax.psum_scatter(
        jnp.dot(activated, down_full, preferred_element_type=jnp.float32).astype(jnp.bfloat16),
        "tensor",
        scatter_dimension=0,
        tiled=True,
    ).astype(jnp.float32)
    second_in = first_out + (ffn_local + down_bias)
    layer_out, second_normed, second_inverse = norm_rows(second_in, second_gain, second_shift)
    upstream = cotangent.astype(jnp.float32) * row_valid[:, None].astype(jnp.float32)
    grad_second, gain_two_part, shift_two_part = norm_back(
        upstream, second_normed, second_inverse, second_gain
    )
    ffn_grad = grad_second.astype(jnp.bfloat16)
    down_bias_part = jnp.sum(ffn_grad.astype(jnp.float32), axis=0)
    qkv_back, out_back, up_back, down_back = (
        lax.all_gather(qkv_weight, "dp", axis=1, tiled=True),
        lax.all_gather(out_weight, "dp", axis=1, tiled=True),
        lax.all_gather(up_weight, "dp", axis=0, tiled=True),
        lax.all_gather(down_weight, "dp", axis=1, tiled=True),
    )
    unused_value, gelu_pull = jax.vjp(gelu_tanh, pre_act)
    seq_ffn_grad = lax.all_gather(ffn_grad, "tensor", axis=0, tiled=True)
    down_grad = jnp.einsum("sf,sd->fd", activated, seq_ffn_grad, preferred_element_type=jnp.float32)
    act_grad = jnp.einsum("sd,fd->sf", seq_ffn_grad, down_back, preferred_element_type=jnp.float32)
    pre_grad = gelu_pull(act_grad)[0].astype(jnp.bfloat16)
    up_bias_part = jnp.sum(pre_grad.astype(jnp.float32), axis=0)
    up_grad = jnp.einsum("sd,sf->df", seq_first, pre_grad, preferred_element_type=jnp.float32)
    first_back = lax.psum_scatter(
        jnp.einsum("sf,df->sd", pre_grad, up_back, preferred_element_type=jnp.float32).astype(
            jnp.bfloat16
        ),
        "tensor",
        scatter_dimension=0,
        tiled=True,
    ).astype(jnp.float32)
    up_grad_full = lax.dynamic_update_slice(
        jnp.zeros((FF,), jnp.float32), up_bias_part, (unit_start,)
    )
    grad_first, gain_one_part, shift_one_part = norm_back(
        grad_second + first_back, first_normed, first_inverse, first_gain
    )
    attn_grad = grad_first.astype(jnp.bfloat16)
    out_bias_part = jnp.sum(attn_grad.astype(jnp.float32), axis=0)
    seq_attn_grad = lax.all_gather(attn_grad, "tensor", axis=0, tiled=True)
    out_grad = jnp.einsum("sc,sd->cd", mixed, seq_attn_grad, preferred_element_type=jnp.float32)
    mixed_grad = jnp.einsum(
        "sd,cd->sc", seq_attn_grad, out_back, preferred_element_type=jnp.float32
    ).astype(jnp.bfloat16)
    mixed_blocks = mixed_grad.reshape(blocks, block, head_count, HEAD)

    def back_block(carry, inputs):
        key_acc, value_acc = carry
        query_block, grad_block, log_total = inputs
        scores = (
            jnp.einsum("qhd,khd->hqk", query_block, key_heads, preferred_element_type=jnp.float32)
            * scale
        )
        scores = jnp.where(key_valid[None, None, :], scores, NEGATIVE)
        probs = jnp.exp(scores - log_total[:, :, None])
        value_acc = value_acc + jnp.einsum(
            "hqk,qhd->khd",
            probs.astype(jnp.bfloat16),
            grad_block,
            preferred_element_type=jnp.float32,
        )
        prob_grad = jnp.einsum(
            "qhd,khd->hqk", grad_block, value_heads, preferred_element_type=jnp.float32
        )
        centre = jnp.sum(probs * prob_grad, axis=-1, keepdims=True)
        score_grad = (probs * (prob_grad - centre)).astype(jnp.bfloat16)
        query_grad = (
            jnp.einsum("hqk,khd->qhd", score_grad, key_heads, preferred_element_type=jnp.float32)
            * scale
        )
        key_acc = (
            key_acc
            + jnp.einsum(
                "hqk,qhd->khd", score_grad, query_block, preferred_element_type=jnp.float32
            )
            * scale
        )
        return ((key_acc, value_acc), query_grad.astype(jnp.bfloat16))

    empty_heads = jnp.zeros((total_rows, head_count, HEAD), jnp.float32)
    (key_total, value_total), query_grads = lax.scan(
        back_block, (empty_heads, empty_heads), (query_blocks, mixed_blocks, log_totals)
    )
    query_grad_rows = query_grads.reshape(total_rows, head_cols)
    key_grad_rows = key_total.reshape(total_rows, head_cols).astype(jnp.bfloat16)
    value_grad_rows = value_total.reshape(total_rows, head_cols).astype(jnp.bfloat16)
    stacked = jnp.stack([query_grad_rows, key_grad_rows, value_grad_rows])
    qkv_grad = jnp.einsum("sd,jsc->jdc", seq_tokens, stacked, preferred_element_type=jnp.float32)
    token_back = lax.psum_scatter(
        jnp.einsum("jsc,jdc->sd", stacked, qkv_back, preferred_element_type=jnp.float32).astype(
            jnp.bfloat16
        ),
        "tensor",
        scatter_dimension=0,
        tiled=True,
    ).astype(jnp.float32)
    grad_tokens = grad_first + token_back
    bias_local = jnp.stack(
        [
            jnp.sum(query_grad_rows.astype(jnp.float32), axis=0),
            jnp.sum(value_grad_rows.astype(jnp.float32), axis=0),
        ]
    )
    qv_grad_full = lax.dynamic_update_slice(
        jnp.zeros((2, D), jnp.float32), bias_local, (jnp.int32(0), head_start)
    )
    grad_qkv, grad_out, grad_up, grad_down = (
        lax.psum_scatter(qkv_grad, "dp", scatter_dimension=1, tiled=True),
        lax.psum_scatter(out_grad, "dp", scatter_dimension=1, tiled=True),
        lax.psum_scatter(up_grad, "dp", scatter_dimension=0, tiled=True),
        lax.psum_scatter(down_grad, "dp", scatter_dimension=1, tiled=True),
    )
    grad_qv, grad_obias, grad_gone, grad_sone, grad_ubias, grad_dbias, grad_gtwo, grad_stwo = (
        lax.psum_scatter(qv_grad_full, ("dp", "tensor"), scatter_dimension=1, tiled=True),
        lax.psum_scatter(out_bias_part, ("dp", "tensor"), scatter_dimension=0, tiled=True),
        lax.psum_scatter(gain_one_part, ("dp", "tensor"), scatter_dimension=0, tiled=True),
        lax.psum_scatter(shift_one_part, ("dp", "tensor"), scatter_dimension=0, tiled=True),
        lax.psum_scatter(up_grad_full, ("dp", "tensor"), scatter_dimension=0, tiled=True),
        lax.psum_scatter(down_bias_part, ("dp", "tensor"), scatter_dimension=0, tiled=True),
        lax.psum_scatter(gain_two_part, ("dp", "tensor"), scatter_dimension=0, tiled=True),
        lax.psum_scatter(shift_two_part, ("dp", "tensor"), scatter_dimension=0, tiled=True),
    )
    return (
        layer_out.astype(jnp.bfloat16),
        grad_tokens,
        grad_qkv,
        grad_qv,
        grad_out,
        grad_obias,
        grad_gone,
        grad_sone,
        grad_up,
        grad_ubias,
        grad_down,
        grad_dbias,
        grad_gtwo,
        grad_stwo,
    )


def solution(mesh):
    return jax.shard_map(
        per_device,
        mesh=mesh,
        in_specs=(
            P(("dp", "tensor"), None),
            P("dp"),
            P(None, "dp", "tensor"),
            P(),
            P("tensor", "dp"),
            P(),
            P(),
            P(),
            P("dp", "tensor"),
            P(),
            P("tensor", "dp"),
            P(),
            P(),
            P(),
            P(("dp", "tensor"), None),
        ),
        out_specs=(
            P(("dp", "tensor"), None),
            P(("dp", "tensor"), None),
            P(None, "dp", "tensor"),
            P(None, ("dp", "tensor")),
            P("tensor", "dp"),
            P(("dp", "tensor")),
            P(("dp", "tensor")),
            P(("dp", "tensor")),
            P("dp", "tensor"),
            P(("dp", "tensor")),
            P("tensor", "dp"),
            P(("dp", "tensor")),
            P(("dp", "tensor")),
            P(("dp", "tensor")),
        ),
        check_vma=False,
    )
```

profile of v0, /device:TPU:0, one launch (start us, length us, event | category | flops | bytes accessed | tf_op | source)
XLA Modules:
  0.0 823.9 jit_solution(12409595684189088999)
XLA Ops:
  11.8 33.1 %all_gather.30 = bf16[192,768]{0,1:T(8,128)(2,1)S(1)} all-gather(bf16[192,96]{0,1:T(8,128)(2,1)S(1)} %copy.46), channel_id=1, replica_groups=mesh['dp'=8,'tensor'=4] {'dp'}, dimensions={1}, use_global_device_ids=true | all-gather | bytes 331776 | tf_op jit(solution)/shard_map/all_gather | solution.py:65
  44.9 38.7 %all_gather.28 = bf16[3,768,192]{2,0,1:T(4,128)(2,1)S(1)} all-gather(bf16[3,96,192]{2,0,1:T(4,128)(2,1)S(1)} %copy.42), channel_id=1, replica_groups=mesh['dp'=8,'tensor'=4] {'dp'}, dimensions={1}, use_global_device_ids=true | all-gather | bytes 995328 | tf_op jit(solution)/shard_map/all_gather | solution.py:64
  95.7 39.1 %while.28 = (s32[]{:T(128)}, bf16[4,512,3,64]{1,3,2,0:T(8,128)(2,1)S(1)}, f32[4,3,512]{2,1,0:T(4,128)}, bf16[4,512,3,64]{1,3,2,0:T(8,128)(2,1)S(1)}, bf16[2048,3...) while((s32[]{:T(128)}, ...), condition=%wide.region_3.4_spmd.clone, body=%wide.region_0.3_spmd.clone.sunk | while | flops 843153920 | bytes 39778412 | solution.py:101
  139.3 36.5 %reduce-scatter.14.cloned.1.call-done = bf16[512,768]{1,0:T(8,128)(2,1)} async-done(((bf16[2048,768]{1,0:T(8,128)(2,1)}), bf16[512,768]{1,0:T(8,128)(2,1)}) %reduce-scatter.14.cloned.1.call-update) | async-done | bytes 786448 | tf_op jit(solution)/shard_map/reduce_scatter | solution.py:104
  183.0 27.5 %all-gather.9.cloned.1.call-done = bf16[2048,768]{1,0:T(8,128)(2,1)} async-done(((bf16[512,768]{1,0:T(8,128)(2,1)}), bf16[2048,768]{1,0:T(8,128)(2,1)}) %all-gather.9.cloned.1.call-update) | async-done | bytes 3145744 | tf_op jit(solution)/shard_map/all_gather | solution.py:111
  210.6 9.7 %fusion.54 = (bf16[2048,768]{1,0:T(8,128)(2,1)}, f32[2048,768]{1,0:T(8,128)}) fusion(f32[768]{0:T(1024)} %dynamic_slice.21, bf16[2048,768]{1,0:T(8,128)(2,1)} %all-gather.9.cloned.1.call-done, bf16[768,768]{1,0:T(8,128)(2,1)} %all-gather.11.cloned.1.call-done), kind=kOutput, calls=%fused_computation.65 | convolution fusion | flops 2431647744 | bytes 13765632 | tf_op jit(solution)/shard_map/dot_general | solution.py:113
  220.2 33.8 %all-gather.13.cloned.1.call-done = bf16[768,768]{0,1:T(8,128)(2,1)} async-done(((bf16[768,96]{0,1:T(8,128)(2,1)}), bf16[768,768]{0,1:T(8,128)(2,1)}) %all-gather.13.cloned.1.call-update) | async-done | bytes 1179664 | tf_op jit(solution)/shard_map/all_gather | solution.py:67
  254.1 6.5 convolution_convert_fusion.1
  261.9 34.9 %reduce-scatter.16.cloned.1.call-done = bf16[512,768]{1,0:T(8,128)(2,1)} async-done(((bf16[2048,768]{1,0:T(8,128)(2,1)}), bf16[512,768]{1,0:T(8,128)(2,1)}) %reduce-scatter.16.cloned.1.call-update) | async-done | bytes 786448 | tf_op jit(solution)/shard_map/reduce_scatter | solution.py:115
  303.9 28.4 %all-gather.15.cloned.1.call-done = bf16[2048,768]{1,0:T(8,128)(2,1)} async-done(((bf16[512,768]{1,0:T(8,128)(2,1)}), bf16[2048,768]{1,0:T(8,128)(2,1)}) %all-gather.15.cloned.1.call-update) | async-done | bytes 3145744 | tf_op jit(solution)/shard_map/all_gather | solution.py:136
  332.3 10.4 %convert_reduce_fusion = (f32[768]{0:T(1024)}, bf16[2048,768]{1,0:T(8,128)(2,1)S(1)}) fusion(f32[2048,768]{1,0:T(8,128)} %get-tuple-element.308, f32[768]{0:T(1024)} %dynamic_slice.21, bf16[2048,768]{1,0:T(8,128)(2,1)} %all-gather.15.cloned.1.call-done, bf16[768,768]{0,1:T(8,128)(2,1)} %all-gather.13.cloned.1.call-done), kind=kOutput, calls=%fused_computation.63 | convolution fusion | flops 2458385664 | bytes 13768704 | tf_op jit(solution)/shard_map/sd,fd->sf/dot_general | solution.py:138
  348.4 37.8 %reduce-scatter.18.cloned.1.call-done = bf16[512,768]{1,0:T(8,128)(2,1)} async-done(((bf16[2048,768]{1,0:T(8,128)(2,1)}), bf16[512,768]{1,0:T(8,128)(2,1)}) %reduce-scatter.18.cloned.1.call-update) | async-done | bytes 786448 | tf_op jit(solution)/shard_map/reduce_scatter | solution.py:142
  392.4 28.6 %all-gather.17.cloned.1.call-done = bf16[2048,768]{1,0:T(8,128)(2,1)} async-done(((bf16[512,768]{1,0:T(8,128)(2,1)}), bf16[2048,768]{1,0:T(8,128)(2,1)}) %all-gather.17.cloned.1.call-update) | async-done | bytes 3145744 | tf_op jit(solution)/shard_map/all_gather | solution.py:158
  435.9 109.8 %while.29 = (s32[]{:T(128)}, f32[2048,3,64]{0,2,1:T(8,128)S(1)}, f32[2048,3,64]{0,2,1:T(8,128)}, bf16[4,512,3,64]{1,3,2,0:T(8,128)(2,1)}, bf16[4,512,3,64]{1,3,2...) while((s32[]{:T(128)}, f32[2048,3,64]{0,2,1:T(8,128)S(1)}, ...), condition=%wide.region_17.18_spmd.clone, body=%wide.region_15.17_spmd.clone.sunk | while | flops 2062615040 | bytes 129222840 | solution.py:199
  454.8 5.6 fusion.138
  482.4 5.7 fusion.138
  537.5 5.6 fusion.138
  563.3 5.8 bitcast_convert_fusion
  569.1 7.1 fusion.76
  576.5 6.9 fusion.77
  584.9 40.3 %all-reduce.8 = (f32[2,768]{1,0:T(2,128)S(1)}, f32[768]{0:T(1024)S(1)}, f32[768]{0:T(1024)S(1)}, f32[768]{0:T(1024)S(1)}, f32[3072]{0:T(1024)S(1)}, /*index=5*/f...) all-reduce(f32[2,768]{1,0:T(2,128)S(1)} %dynamic_update_slice.17, ...), channel_id=7, replica_groups=mesh['dp'=8,'tensor'=4] {'dp','tensor'}, use_global_device_ids=true, to_apply=%region_22.23.clone | all-reduce | flops 9216 | bytes 73728
  633.4 36.3 %reduce-scatter.20.cloned.1.call-done = bf16[512,768]{1,0:T(8,128)(2,1)} async-done(((bf16[2048,768]{1,0:T(8,128)(2,1)}), bf16[512,768]{1,0:T(8,128)(2,1)}) %reduce-scatter.20.cloned.1.call-update) | async-done | bytes 786448 | tf_op jit(solution)/shard_map/reduce_scatter | solution.py:207
  672.2 71.3 %reduce-scatter.22.cloned.1.call-done = f32[96,768]{1,0:T(8,128)} async-done(((f32[768,768]{1,0:T(8,128)}), f32[96,768]{1,0:T(8,128)}) %reduce-scatter.22.cloned.1.call-update) | async-done | bytes 294928 | tf_op jit(solution)/shard_map/reduce_scatter | solution.py:228
  743.5 73.1 %reduce-scatter.24.cloned.1.call-done = f32[768,96]{0,1:T(8,128)} async-done(((f32[768,768]{0,1:T(8,128)}), f32[768,96]{0,1:T(8,128)}) %reduce-scatter.24.cloned.1.call-update) | async-done | bytes 294928 | tf_op jit(solution)/shard_map/reduce_scatter | solution.py:229
  (216 shorter events, 223.3 us)
Async XLA Ops:
  8.0 75.6 %all-gather.7.cloned.1.call-start = ((), (), s32[]{:S(2)}) async-start(), calls=%async_computation.8 | async-start | bytes 3932160 | tf_op jit(solution)/shard_map/all_gather | solution.py:69
  8.7 167.1 %reduce-scatter.14.cloned.1.call-start = ((), (), s32[]{:S(2)}) async-start(), calls=%async_computation.9 | async-start | bytes 3932160 | tf_op jit(solution)/shard_map/reduce_scatter | solution.py:104
  138.5 37.3 %copy-start.1 = (bf16[512,768]{1,0:T(8,128)(2,1)S(1)}, bf16[512,768]{1,0:T(8,128)(2,1)}, u32[]{:S(2)}) copy-start(bf16[512,768]{1,0:T(8,128)(2,1)} %param.19) | copy-start | bytes 2359300
  138.5 37.3 %copy-start.16 = (f32[768]{0:T(1024)S(1)}, f32[768]{0:T(1024)}, u32[]{:S(2)}) copy-start(f32[768]{0:T(1024)} %param.24) | copy-start | bytes 9220
  138.5 40.4 %copy-start.17 = (f32[768]{0:T(1024)S(1)}, f32[768]{0:T(1024)}, u32[]{:S(2)}) copy-start(f32[768]{0:T(1024)} %param.25) | copy-start | bytes 9220
  138.5 44.5 %all-gather.11.cloned.1.call-start = ((), (), s32[]{:S(2)}) async-start(), calls=%async_computation.11 | async-start | bytes 1327104 | tf_op jit(solution)/shard_map/all_gather | solution.py:66
  139.1 71.5 %all-gather.9.cloned.1.call-start = ((), (), s32[]{:S(2)}) async-start(), calls=%async_computation.10 | async-start | bytes 3932160 | tf_op jit(solution)/shard_map/all_gather | solution.py:111
  181.0 73.1 %all-gather.13.cloned.1.call-start = ((), (), s32[]{:S(2)}) async-start(), calls=%async_computation.12 | async-start | bytes 1327104 | tf_op jit(solution)/shard_map/all_gather | solution.py:67
  181.6 115.2 %reduce-scatter.16.cloned.1.call-start = ((), (), s32[]{:S(2)}) async-start(), calls=%async_computation.13 | async-start | bytes 3932160 | tf_op jit(solution)/shard_map/reduce_scatter | solution.py:115
  260.6 71.7 %all-gather.15.cloned.1.call-start = ((), (), s32[]{:S(2)}) async-start(), calls=%async_computation.14 | async-start | bytes 3932160 | tf_op jit(solution)/shard_map/all_gather | solution.py:136
  303.6 82.6 %reduce-scatter.18.cloned.1.call-start = ((), (), s32[]{:S(2)}) async-start(), calls=%async_computation.15 | async-start | bytes 3932160 | tf_op jit(solution)/shard_map/reduce_scatter | solution.py:142
  332.3 12.1 %copy-start.28 = (bf16[768,768]{1,0:T(8,128)(2,1)S(1)}, bf16[768,768]{1,0:T(8,128)(2,1)}, u32[]{:S(2)}) copy-start(bf16[768,768]{1,0:T(8,128)(2,1)} %all-gather.11.cloned.1.call-done) | copy-start | bytes 3538948
  348.4 72.6 %all-gather.17.cloned.1.call-start = ((), (), s32[]{:S(2)}) async-start(), calls=%async_computation.16 | async-start | bytes 3932160 | tf_op jit(solution)/shard_map/all_gather | solution.py:158
  392.3 237.6 %reduce-scatter.28.cloned.1.call-start = ((), (), s32[]{:S(2)}) async-start(), calls=%async_computation.21 | async-start | bytes 884736
  434.5 197.1 %reduce-scatter.26.cloned.1.call-start = ((), (), s32[]{:S(2)}) async-start(), calls=%async_computation.20 | async-start | bytes 2211840
  454.8 5.6 copy-start
  482.4 5.7 copy-start
  510.0 5.6 copy-start
  537.5 5.6 copy-start
  558.4 4.9 copy-start.12
  563.2 106.6 %reduce-scatter.20.cloned.1.call-start = ((), (), s32[]{:S(2)}) async-start(), calls=%async_computation.17 | async-start | bytes 3932160 | tf_op jit(solution)/shard_map/reduce_scatter | solution.py:207
  569.1 174.4 %reduce-scatter.22.cloned.1.call-start = ((), (), s32[]{:S(2)}) async-start(), calls=%async_computation.18 | async-start | bytes 2654208 | tf_op jit(solution)/shard_map/reduce_scatter | solution.py:228
  576.3 240.3 %reduce-scatter.24.cloned.1.call-start = ((), (), s32[]{:S(2)}) async-start(), calls=%async_computation.19 | async-start | bytes 2654208 | tf_op jit(solution)/shard_map/reduce_scatter | solution.py:229
  583.5 86.3 %copy-start.7 = (f32[512,768]{1,0:T(8,128)S(1)}, f32[512,768]{1,0:T(8,128)}, u32[]{:S(2)}) copy-start(f32[512,768]{1,0:T(8,128)} %get-tuple-element.295) | copy-start | bytes 4718596
  (23 other events, 43.8 us)
Sparse Core Ops, SparseCore 0:
  10.4 31.2 all-gather.6
  138.6 37.1 reduce-scatter.13
  303.7 28.5 all-gather.14
  392.5 28.4 all-gather.16
Sparse Core Ops, SparseCore 1:
  141.2 40.5 all-gather.10
  183.8 26.7 all-gather.8
  212.6 41.4 all-gather.12
  260.7 36.0 reduce-scatter.15
  348.5 37.7 reduce-scatter.17
  434.6 63.3 reduce-scatter.27
  563.3 67.3 reduce-scatter.25
  633.1 36.6 reduce-scatter.19
  673.7 69.7 reduce-scatter.21
  747.6 68.9 reduce-scatter.23
where the time goes:
time: 834 us; the launch traced here: 824 us
  waiting for transfers between devices  410 us (49%)
  matrix products  177 us (21%)
  blocking collectives  112 us (13%)
  other arithmetic  64.9 us (8%)
  local copies, waits for them, and re-layouts  41.4 us (5%)
  between operations  16.6 us (2%)
    reduce_scatter x1, waiting for transfers between devices, per_device(): lax.psum_scatter(down_grad, 'dp', scatter_dimension=1, tiled=True)  73.1 us
    reduce_scatter x1, waiting for transfers between devices, per_device(): lax.psum_scatter(up_grad, 'dp', scatter_dimension=0, tiled=True)  71.3 us
    unnamed x1, blocking collectives  40.3 us
    all_gather x1, blocking collectives, per_device(): lax.all_gather(qkv_weight, 'dp', axis=1, tiled=True)  38.7 us
    reduce_scatter x1, waiting for transfers between devices, per_device(): lax.psum_scatter(jnp.einsum('sf,df->sd', pre_grad, up_back, preferred_ele...  37.8 us
    reduce_scatter x1, waiting for transfers between devices, per_device(): lax.psum_scatter(out_part.astype(jnp.bfloat16), 'tensor', scatter_dimensi...  36.5 us
    reduce_scatter x1, waiting for transfers between devices, per_device(): lax.psum_scatter(jnp.einsum('jsc,jdc->sd', stacked, qkv_back, preferred_e...  36.3 us
    reduce_scatter x1, waiting for transfers between devices, per_device(): lax.psum_scatter(jnp.dot(activated, down_full, preferred_element_type=jnp...  34.9 us
  transfers between devices with their start and end apart: 14, of which 10 were waited for; matrix products, arithmetic and copies ran while one was open for 22% of the time, Pallas kernels for 0%

commit v1 on v0

v1 whole, which is shorter than its diff:
```python
import math

import jax
import jax.numpy as jnp
from jax import lax
from jax.sharding import PartitionSpec as P

HEAD = 64
NEGATIVE = -1e30
EPSILON = 1e-05
F32 = jnp.float32
BF16 = jnp.bfloat16


def gelu_tanh(values):
    bracket = 0.7978845608028654 * (values + 0.044715 * values * values * values)
    return 0.5 * values * (1.0 + jnp.tanh(bracket))


def norm_rows(hidden, scaling, offset):
    centered = hidden - jnp.mean(hidden, axis=-1, keepdims=True)
    inverse = lax.rsqrt(jnp.mean(centered * centered, axis=-1, keepdims=True) + EPSILON)
    normed = centered * inverse
    return (normed * scaling + offset, normed, inverse)


def norm_back(upstream, normed, inverse, scaling):
    scaled = upstream * scaling
    bracket = (
        scaled
        - jnp.mean(scaled, axis=-1, keepdims=True)
        - normed * jnp.mean(scaled * normed, axis=-1, keepdims=True)
    )
    return (inverse * bracket, jnp.sum(upstream * normed, axis=0), jnp.sum(upstream, axis=0))


def mm(left, right, dims):
    return lax.dot_general(left, right, (dims, ((), ())), preferred_element_type=F32)


def gather_tensor(rows):
    return lax.all_gather(rows, "tensor", axis=0, tiled=True)


def scatter_tensor(part):
    return lax.psum_scatter(part, "tensor", scatter_dimension=0, tiled=True)


def attention_forward(queries, key_rows, value_rows, length):
    total_rows, head_cols = queries.shape
    head_count = head_cols // HEAD
    scale = 1.0 / math.sqrt(HEAD)
    block = min(512, total_rows)
    blocks = total_rows // block
    key_valid = jnp.arange(total_rows, dtype=jnp.int32) < length
    key_heads = key_rows.reshape(total_rows, head_count, HEAD)
    value_heads = value_rows.reshape(total_rows, head_count, HEAD)
    query_blocks = queries.reshape(blocks, block, head_count, HEAD)

    def attend_block(query_block):
        scores = (
            jnp.einsum("qhd,khd->hqk", query_block, key_heads, preferred_element_type=F32) * scale
        )
        scores = jnp.where(key_valid[None, None, :], scores, NEGATIVE)
        top_score = jnp.max(scores, axis=-1, keepdims=True)
        expo = jnp.exp(scores - top_score)
        row_total = jnp.sum(expo, axis=-1, keepdims=True)
        probs = (expo / row_total).astype(BF16)
        context = jnp.einsum("hqk,khd->qhd", probs, value_heads, preferred_element_type=F32)
        return (context.astype(BF16), (top_score + jnp.log(row_total))[..., 0])

    context_blocks, log_totals = lax.map(attend_block, query_blocks)
    return context_blocks.reshape(total_rows, head_cols), log_totals


def attention_backward(queries, key_rows, value_rows, mixed_grad, log_totals, length):
    total_rows, head_cols = queries.shape
    head_count = head_cols // HEAD
    scale = 1.0 / math.sqrt(HEAD)
    block = min(512, total_rows)
    blocks = total_rows // block
    key_valid = jnp.arange(total_rows, dtype=jnp.int32) < length
    key_heads = key_rows.reshape(total_rows, head_count, HEAD)
    value_heads = value_rows.reshape(total_rows, head_count, HEAD)
    query_blocks = queries.reshape(blocks, block, head_count, HEAD)
    mixed_blocks = mixed_grad.reshape(blocks, block, head_count, HEAD)

    def back_block(carry, inputs):
        key_acc, value_acc = carry
        query_block, grad_block, log_total = inputs
        scores = (
            jnp.einsum("qhd,khd->hqk", query_block, key_heads, preferred_element_type=F32) * scale
        )
        scores = jnp.where(key_valid[None, None, :], scores, NEGATIVE)
        probs = jnp.exp(scores - log_total[:, :, None])
        value_acc = value_acc + jnp.einsum(
            "hqk,qhd->khd", probs.astype(BF16), grad_block, preferred_element_type=F32
        )
        prob_grad = jnp.einsum("qhd,khd->hqk", grad_block, value_heads, preferred_element_type=F32)
        centre = jnp.sum(probs * prob_grad, axis=-1, keepdims=True)
        score_grad = (probs * (prob_grad - centre)).astype(BF16)
        query_grad = (
            jnp.einsum("hqk,khd->qhd", score_grad, key_heads, preferred_element_type=F32) * scale
        )
        key_acc = (
            key_acc
            + jnp.einsum("hqk,qhd->khd", score_grad, query_block, preferred_element_type=F32)
            * scale
        )
        return ((key_acc, value_acc), query_grad.astype(BF16))

    empty = jnp.zeros((total_rows, head_count, HEAD), F32)
    (key_total, value_total), query_grads = lax.scan(
        back_block, (empty, empty), (query_blocks, mixed_blocks, log_totals)
    )
    return (
        query_grads.reshape(total_rows, head_cols),
        key_total.reshape(total_rows, head_cols).astype(BF16),
        value_total.reshape(total_rows, head_cols).astype(BF16),
    )


def per_device(
    tokens,
    lengths,
    qkv_weight,
    qv_bias,
    out_weight,
    out_bias,
    first_gain,
    first_shift,
    up_weight,
    up_bias,
    down_weight,
    down_bias,
    second_gain,
    second_shift,
    cotangent,
):
    local_rows, width = tokens.shape
    piece = lax.axis_index("tensor")
    ways = lax.axis_size("dp") * lax.axis_size("tensor")
    head_cols = qkv_weight.shape[2]
    unit_cols = up_weight.shape[1]
    depth = up_weight.shape[0]
    length = lengths[0]
    qkv_rows = jnp.concatenate([qkv_weight[0], qkv_weight[1], qkv_weight[2]], axis=1)
    qkv_full = lax.all_gather(qkv_rows, "dp", axis=0, tiled=True)
    rest_rows = jnp.concatenate([up_weight, down_weight.T, out_weight.T], axis=1)
    rest_full = lax.all_gather(rest_rows, "dp", axis=0, tiled=True)
    up_full = rest_full[:, :unit_cols]
    down_full = rest_full[:, unit_cols : 2 * unit_cols]
    out_full = rest_full[:, 2 * unit_cols :]
    seq_tokens = gather_tensor(tokens)
    row_start = piece * local_rows
    row_valid = row_start + jnp.arange(local_rows, dtype=jnp.int32) < length
    head_start = piece * head_cols
    unit_start = piece * unit_cols
    bias_cols = lax.dynamic_slice_in_dim(qv_bias, head_start, head_cols, 1)
    qkv_bias = jnp.concatenate([bias_cols[0], jnp.zeros((head_cols,), F32), bias_cols[1]])
    projected = (mm(seq_tokens, qkv_full, ((1,), (0,))) + qkv_bias).astype(BF16)
    queries = projected[:, :head_cols]
    key_rows = projected[:, head_cols : 2 * head_cols]
    value_rows = projected[:, 2 * head_cols :]
    mixed, log_totals = attention_forward(queries, key_rows, value_rows, length)
    attn_local = scatter_tensor(mm(mixed, out_full, ((1,), (1,))).astype(BF16)).astype(F32)
    first_out, first_normed, first_inverse = norm_rows(
        tokens.astype(F32) + (attn_local + out_bias), first_gain, first_shift
    )
    seq_first = gather_tensor(first_out.astype(BF16))
    up_cols = lax.dynamic_slice_in_dim(up_bias, unit_start, unit_cols, 0)
    pre_act = mm(seq_first, up_full, ((1,), (0,))) + up_cols
    activated = gelu_tanh(pre_act).astype(BF16)
    ffn_local = scatter_tensor(mm(activated, down_full, ((1,), (1,))).astype(BF16)).astype(F32)
    second_in = first_out + (ffn_local + down_bias)
    layer_out, second_normed, second_inverse = norm_rows(second_in, second_gain, second_shift)
    upstream = cotangent.astype(F32) * row_valid[:, None].astype(F32)
    grad_second, gain_two_part, shift_two_part = norm_back(
        upstream, second_normed, second_inverse, second_gain
    )
    ffn_grad = grad_second.astype(BF16)
    down_bias_part = jnp.sum(ffn_grad.astype(F32), axis=0)
    unused_value, gelu_pull = jax.vjp(gelu_tanh, pre_act)
    seq_ffn_grad = gather_tensor(ffn_grad)
    act_grad = mm(seq_ffn_grad, down_full, ((1,), (0,)))
    pre_grad = gelu_pull(act_grad)[0].astype(BF16)
    first_back = scatter_tensor(mm(pre_grad, up_full, ((1,), (1,))).astype(BF16)).astype(F32)
    up_bias_part = jnp.sum(pre_grad.astype(F32), axis=0)
    down_grad = mm(seq_ffn_grad, activated, ((0,), (0,))).astype(BF16)
    up_grad = mm(seq_first, pre_grad, ((0,), (0,))).astype(BF16)
    grad_first, gain_one_part, shift_one_part = norm_back(
        grad_second + first_back, first_normed, first_inverse, first_gain
    )
    attn_grad = grad_first.astype(BF16)
    out_bias_part = jnp.sum(attn_grad.astype(F32), axis=0)
    attn_grad, up_grad, down_grad = lax.optimization_barrier((attn_grad, up_grad, down_grad))
    grad_ud = lax.psum_scatter(
        jnp.concatenate([up_grad, down_grad], axis=1), "dp", scatter_dimension=0, tiled=True
    )
    seq_attn_grad = gather_tensor(attn_grad)
    out_grad = mm(seq_attn_grad, mixed, ((0,), (0,))).astype(BF16)
    mixed_grad = mm(seq_attn_grad, out_full, ((1,), (0,))).astype(BF16)
    query_grad, key_grad, value_grad = attention_backward(
        queries, key_rows, value_rows, mixed_grad, log_totals, length
    )
    stacked = jnp.concatenate([query_grad, key_grad, value_grad], axis=1)
    token_back = scatter_tensor(mm(stacked, qkv_full, ((1,), (1,))).astype(BF16)).astype(F32)
    qkv_grad = mm(seq_tokens, stacked, ((0,), (0,))).astype(BF16)
    grad_qo = lax.psum_scatter(
        jnp.concatenate([qkv_grad, out_grad], axis=1), "dp", scatter_dimension=0, tiled=True
    )
    grad_tokens = grad_first + token_back
    zeros_heads = jnp.zeros((width,), F32)
    query_bias = lax.dynamic_update_slice(
        zeros_heads, jnp.sum(query_grad.astype(F32), axis=0), (head_start,)
    )
    value_bias = lax.dynamic_update_slice(
        zeros_heads, jnp.sum(value_grad.astype(F32), axis=0), (head_start,)
    )
    up_bias_full = lax.dynamic_update_slice(
        jnp.zeros((up_bias.shape[0],), F32), up_bias_part, (unit_start,)
    )
    small = jnp.concatenate(
        [
            item.reshape(ways, -1)
            for item in (
                query_bias,
                value_bias,
                out_bias_part,
                gain_one_part,
                shift_one_part,
                up_bias_full,
                down_bias_part,
                gain_two_part,
                shift_two_part,
            )
        ],
        axis=1,
    )
    small = lax.psum_scatter(small, ("dp", "tensor"), scatter_dimension=0, tiled=True)[0]
    share = width // ways
    cuts = [0]
    for size in (share, share, share, share, share, up_bias.shape[0] // ways, share, share, share):
        cuts.append(cuts[-1] + size)
    bits = [small[cuts[i] : cuts[i + 1]] for i in range(9)]
    grad_ud = grad_ud.astype(F32)
    grad_qo = grad_qo.astype(F32)
    grad_qkv = jnp.stack([grad_qo[:, i * head_cols : (i + 1) * head_cols] for i in range(3)])
    return (
        layer_out.astype(BF16),
        grad_tokens,
        grad_qkv,
        jnp.stack([bits[0], bits[1]]),
        grad_qo[:, 3 * head_cols :].T,
        bits[2],
        bits[3],
        bits[4],
        grad_ud[:, :unit_cols],
        bits[5],
        grad_ud[:, unit_cols:].T,
        bits[6],
        bits[7],
        bits[8],
    )


def solution(mesh):
    both = ("dp", "tensor")
    return jax.shard_map(
        per_device,
        mesh=mesh,
        in_specs=(
            P(both, None),
            P("dp"),
            P(None, "dp", "tensor"),
            P(),
            P("tensor", "dp"),
            P(),
            P(),
            P(),
            P("dp", "tensor"),
            P(),
            P("tensor", "dp"),
            P(),
            P(),
            P(),
            P(both, None),
        ),
        out_specs=(
            P(both, None),
            P(both, None),
            P(None, "dp", "tensor"),
            P(None, both),
            P("tensor", "dp"),
            P(both),
            P(both),
            P(both),
            P("dp", "tensor"),
            P(both),
            P("tensor", "dp"),
            P(both),
            P(both),
            P(both),
        ),
        check_vma=False,
    )
```

time: 834 us -> 600 us (0.72)
  waiting for transfers between devices: 410 us -> 237 us
  blocking collectives: 112 us -> 74.5 us
  local copies, waits for them, and re-layouts: 41.4 us -> 27.9 us
    reduce_scatter x6 -> x5, waiting for transfers between devices: 290 us -> 134 us  [the longest x4 134 us: scatter_tensor(): return lax.psum_scatter(part, 'tensor', scatter_dimension=0, tiled=True)]
    all_gather x2 -> x1, blocking collectives: 71.8 us -> 34.7 us  [per_device(): qkv_full = lax.all_gather(qkv_rows, 'dp', axis=0, tiled=True)]
    all_gather x6 -> x5, waiting for transfers between devices: 118 us -> 90.2 us  [the longest x4 81.1 us: gather_tensor(): return lax.all_gather(rows, 'tensor', axis=0, tiled=True)]
    unnamed x75 -> x72, local copies, waits for them, and re-layouts: 25.2 us -> 12 us
    unnamed x16 -> x12, waiting for transfers between devices: 1.91 us -> 12.4 us
    dot_general x19 -> x20, matrix products: 102 us -> 98.6 us  [the longest x12 62.3 us: mm(): lax.dot_general(left, right, (dims, ((), ())), preferred_element_type=F32)]
  transfers between devices with their start and end apart: 14 -> 11, of which waited for: 10 -> 9; matrix products, arithmetic and copies ran while one was open for 22% -> 35% of each run, Pallas kernels for 0% -> 0%
where the time goes in v1:
time: 600 us; the launch traced here: 591 us
  waiting for transfers between devices  237 us (40%)
  matrix products  169 us (28%)
  blocking collectives  74.5 us (12%)
  other arithmetic  64.9 us (11%)
  local copies, waits for them, and re-layouts  27.9 us (5%)
  between operations  15.6 us (3%)
    reduce_scatter x4, waiting for transfers between devices, scatter_tensor(): return lax.psum_scatter(part, 'tensor', scatter_dimension=0, tiled=True)  134 us
    all_gather x4, waiting for transfers between devices, gather_tensor(): return lax.all_gather(rows, 'tensor', axis=0, tiled=True)  81.1 us
    dot_general x12, matrix products, mm(): lax.dot_general(left, right, (dims, ((), ())), preferred_element_type=F32)  62.3 us
    unnamed x1, blocking collectives  39.8 us
    all_gather x1, blocking collectives, per_device(): qkv_full = lax.all_gather(qkv_rows, 'dp', axis=0, tiled=True)  34.7 us
    dot_general x4, matrix products, back_block(): jnp.einsum('hqk,khd->qhd', score_grad, key_heads, preferred_element_type=...  22.6 us
    dot_general x4, matrix products, back_block(): jnp.einsum('hqk,qhd->khd', probs.astype(BF16), grad_block, preferred_elem...  21.6 us
    convert_element_type x4, other arithmetic, back_block(): score_grad = (probs * (prob_grad - centre)).astype(BF16)  19.7 us
  transfers between devices with their start and end apart: 11, of which 9 were waited for; matrix products, arithmetic and copies ran while one was open for 35% of the time, Pallas kernels for 0%

profile of v1, /device:TPU:0, one launch (start us, length us, event | category | flops | bytes accessed | tf_op | source)
XLA Modules:
  0.0 590.7 jit_solution(8400919664142980488)
XLA Ops:
  11.7 34.7 %all_gather.18 = bf16[768,576]{1,0:T(8,128)(2,1)S(1)} all-gather(bf16[96,576]{1,0:T(8,128)(2,1)S(1)} %pad_maximum_fusion.7), channel_id=1, replica_groups=mesh['dp'=8,'tensor'=4] {'dp'}, dimensions={0}, use_global_device_ids=true | all-gather | bytes 995328 | tf_op jit(solution)/shard_map/all_gather | solution.py:148
  52.7 36.8 %while.28 = (s32[]{:T(128)}, bf16[4,512,3,64]{1,3,2,0:T(8,128)(2,1)S(1)}, f32[4,3,512]{2,1,0:T(4,128)S(1)}, bf16[4,512,3,64]{1,3,2,0:T(8,128)(2,1)S(1)}, bf16[20...) while((s32[]{:T(128)}, ...), condition=%wide.region_3.4_spmd.clone, body=%wide.region_0.3_spmd.clone.sunk | while | flops 843153920 | bytes 39782508 | solution.py:72
  90.2 9.1 %all-gather.8.cloned.1.call-done = bf16[768,1728]{1,0:T(8,128)(2,1)} async-done(((bf16[96,1728]{1,0:T(8,128)(2,1)}), bf16[768,1728]{1,0:T(8,128)(2,1)}) %all-gather.8.cloned.1.call-update) | async-done | bytes 2654224 | tf_op jit(solution)/shard_map/all_gather | solution.py:150
  103.3 36.7 %reduce-scatter.9.cloned.1.call-done = bf16[512,768]{1,0:T(8,128)(2,1)} async-done(((bf16[2048,768]{1,0:T(8,128)(2,1)}), bf16[512,768]{1,0:T(8,128)(2,1)}) %reduce-scatter.9.cloned.1.call-update) | async-done | bytes 786448 | tf_op jit(solution)/shard_map/reduce_scatter | solution.py:46
  145.8 27.4 %all-gather.10.cloned.1.call-done = bf16[2048,768]{1,0:T(8,128)(2,1)} async-done(((bf16[512,768]{1,0:T(8,128)(2,1)}), bf16[2048,768]{1,0:T(8,128)(2,1)}) %all-gather.10.cloned.1.call-update) | async-done | bytes 3145744 | tf_op jit(solution)/shard_map/all_gather | solution.py:42
  180.8 6.7 %convolution_convert_fusion.2 = bf16[2048,768]{1,0:T(8,128)(2,1)} fusion(bf16[768,1728]{1,0:T(8,128)(2,1)} %all-gather.8.cloned.1.call-done, f32[2048,768]{1,0:T(8,128)S(1)} %fusion.68, f32[768]{0:T(1024)S(1)} %dynamic_slice.21), kind=kOutput, calls=%fused_computation.68 | convolution fusion | flops 2433220608 | bytes 10619904 | tf_op jit(solution)/shard_map/dot_general | solution.py:38
  188.3 37.3 %reduce-scatter.11.cloned.1.call-done = bf16[512,768]{1,0:T(8,128)(2,1)} async-done(((bf16[2048,768]{1,0:T(8,128)(2,1)}), bf16[512,768]{1,0:T(8,128)(2,1)}) %reduce-scatter.11.cloned.1.call-update) | async-done | bytes 786448 | tf_op jit(solution)/shard_map/reduce_scatter | solution.py:46
  232.4 28.6 %all-gather.12.cloned.1.call-done = bf16[2048,768]{1,0:T(8,128)(2,1)} async-done(((bf16[512,768]{1,0:T(8,128)(2,1)}), bf16[2048,768]{1,0:T(8,128)(2,1)}) %all-gather.12.cloned.1.call-update) | async-done | bytes 3145744 | tf_op jit(solution)/shard_map/all_gather | solution.py:42
  261.0 10.3 %convert_reduce_fusion = (f32[768]{0:T(1024)}, bf16[2048,768]{1,0:T(8,128)(2,1)S(1)}) fusion(f32[2048,768]{1,0:T(8,128)} %copy-done.32, f32[768]{0:T(1024)S(1)} %dynamic_slice.21, bf16[2048,768]{1,0:T(8,128)(2,1)} %all-gather.12.cloned.1.call-done, bf16[768,1728]{1,0:T(8,128)(2,1)} %all-gather.8.cloned.1.call-done), kind=kOutput, calls=%fused_computation.62 | convolution fusion | flops 2458385664 | bytes 13768704 | tf_op jit(solution)/shard_map/dot_general | solution.py:38
  278.6 6.8 %convolution_convert_fusion.6 = bf16[768,768]{1,0:T(8,128)(2,1)} fusion(bf16[2048,768]{1,0:T(8,128)(2,1)} %all-gather.10.cloned.1.call-done, bf16[2048,768]{1,0:T(8,128)(2,1)} %copy-done.31), kind=kOutput, calls=%fused_computation.97 | convolution fusion | flops 2416508928 | bytes 7471104 | tf_op jit(solution)/shard_map/dot_general | solution.py:38
  285.3 7.5 %convolution_convert_fusion.5 = bf16[768,768]{1,0:T(8,128)(2,1)} fusion(bf16[2048,768]{1,0:T(8,128)(2,1)S(1)} %copy-done.30, f32[2048,768]{1,0:T(8,128)} %copy-done.32, f32[768]{0:T(1024)S(1)} %dynamic_slice.21), kind=kOutput, calls=%fused_computation.96 | convolution fusion | flops 2432237568 | bytes 10619904 | tf_op jit(solution)/shard_map/dot_general | solution.py:38
  292.9 23.5 %reduce-scatter.13.cloned.1.call-done = bf16[512,768]{1,0:T(8,128)(2,1)} async-done(((bf16[2048,768]{1,0:T(8,128)(2,1)}), bf16[512,768]{1,0:T(8,128)(2,1)}) %reduce-scatter.13.cloned.1.call-update) | async-done | bytes 786448 | tf_op jit(solution)/shard_map/reduce_scatter | solution.py:46
  326.1 25.1 %all-gather.14.cloned.1.call-done = bf16[2048,768]{1,0:T(8,128)(2,1)} async-done(((bf16[512,768]{1,0:T(8,128)(2,1)}), bf16[2048,768]{1,0:T(8,128)(2,1)}) %all-gather.14.cloned.1.call-update) | async-done | bytes 3145744 | tf_op jit(solution)/shard_map/all_gather | solution.py:42
  361.4 106.9 %while.29 = (s32[]{:T(128)}, f32[2048,3,64]{0,2,1:T(8,128)S(1)}, f32[2048,3,64]{0,2,1:T(8,128)}, bf16[4,512,3,64]{1,3,2,0:T(8,128)(2,1)}, bf16[4,512,3,64]{1,3,2...) while((s32[]{:T(128)}, f32[2048,3,64]{0,2,1:T(8,128)S(1)}, ...), condition=%wide.region_17.18_spmd.clone, body=%wide.region_15.17_spmd.clone.sunk | while | flops 2062615040 | bytes 129222840 | solution.py:113
  379.6 5.7 fusion.136
  391.1 5.5 fusion.135
  406.5 5.6 fusion.136
  417.9 5.6 fusion.135
  433.3 5.6 fusion.136
  460.1 5.6 fusion.136
  477.0 5.7 convolution_convert_fusion
  488.0 39.8 %all-reduce = f32[32,288]{1,0:T(8,128)S(1)} all-reduce(f32[32,288]{1,0:T(8,128)S(1)} %concatenate.26), channel_id=7, replica_groups=mesh['dp'=8,'tensor'=4] {'dp','tensor'}, use_global_device_ids=true, to_apply=%region_29.30.clone | all-reduce | flops 9216 | bytes 73728
  530.3 11.6 %reduce-scatter.19.cloned.1.call-done = bf16[96,768]{1,0:T(8,128)(2,1)} async-done(((bf16[768,768]{1,0:T(8,128)(2,1)}), bf16[96,768]{1,0:T(8,128)(2,1)}) %reduce-scatter.19.cloned.1.call-update) | async-done | bytes 147472
  544.6 36.7 %reduce-scatter.15.cloned.1.call-done = bf16[512,768]{1,0:T(8,128)(2,1)} async-done(((bf16[2048,768]{1,0:T(8,128)(2,1)}), bf16[512,768]{1,0:T(8,128)(2,1)}) %reduce-scatter.15.cloned.1.call-update) | async-done | bytes 786448 | tf_op jit(solution)/shard_map/reduce_scatter | solution.py:46
  (224 shorter events, 193.3 us)
Async XLA Ops:
  7.2 40.1 %all-gather.6.cloned.1.call-start = ((), (), s32[]{:S(2)}) async-start(), calls=%async_computation.6 | async-start | bytes 3932160 | tf_op jit(solution)/shard_map/all_gather | solution.py:42
  7.9 91.5 %all-gather.8.cloned.1.call-start = ((), (), s32[]{:S(2)}) async-start(), calls=%async_computation.7 | async-start | bytes 3096576 | tf_op jit(solution)/shard_map/all_gather | solution.py:150
  10.6 129.4 %reduce-scatter.9.cloned.1.call-start = ((), (), s32[]{:S(2)}) async-start(), calls=%async_computation.8 | async-start | bytes 3932160 | tf_op jit(solution)/shard_map/reduce_scatter | solution.py:46
  89.4 10.0 %copy-start.3 = (bf16[4,512,3,64]{1,3,2,0:T(8,128)(2,1)}, bf16[4,512,3,64]{1,3,2,0:T(8,128)(2,1)S(1)}, u32[]{:S(2)}) copy-start(bf16[4,512,3,64]{1,3,2,0:T(8,128)(2,1)S(1)} %get-tuple-element.532) | copy-start | bytes 2359300
  90.2 13.0 %copy-start.7 = (bf16[24,8,4,512]{3,1,2,0:T(8,128)(2,1)}, bf16[24,8,4,512]{3,1,2,0:T(8,128)(2,1)S(1)}, u32[]{:S(2)}) copy-start(bf16[24,8,4,512]{3,1,2,0:T(8,128)(2,1)S(1)} %copy.50) | copy-start | bytes 2359300
  99.4 40.6 %copy-start.1 = (bf16[512,768]{1,0:T(8,128)(2,1)S(1)}, bf16[512,768]{1,0:T(8,128)(2,1)}, u32[]{:S(2)}) copy-start(bf16[512,768]{1,0:T(8,128)(2,1)} %param.19) | copy-start | bytes 2359300
  99.4 40.6 %copy-start.16 = (f32[768]{0:T(1024)S(1)}, f32[768]{0:T(1024)}, u32[]{:S(2)}) copy-start(f32[768]{0:T(1024)} %param.24) | copy-start | bytes 9220
  103.2 40.0 %copy-start.17 = (f32[768]{0:T(1024)S(1)}, f32[768]{0:T(1024)}, u32[]{:S(2)}) copy-start(f32[768]{0:T(1024)} %param.25) | copy-start | bytes 9220
  103.2 40.0 %copy-start.20 = (f32[768]{0:T(1024)S(1)}, f32[768]{0:T(1024)}, u32[]{:S(2)}) copy-start(f32[768]{0:T(1024)} %param.26) | copy-start | bytes 9220
  103.2 70.0 %all-gather.10.cloned.1.call-start = ((), (), s32[]{:S(2)}) async-start(), calls=%async_computation.9 | async-start | bytes 3932160 | tf_op jit(solution)/shard_map/all_gather | solution.py:42
  144.5 81.0 %reduce-scatter.11.cloned.1.call-start = ((), (), s32[]{:S(2)}) async-start(), calls=%async_computation.10 | async-start | bytes 3932160 | tf_op jit(solution)/shard_map/reduce_scatter | solution.py:46
  187.5 38.1 %copy-start.27 = (f32[768]{0:T(1024)S(1)}, f32[768]{0:T(1024)}, u32[]{:S(2)}) copy-start(f32[768]{0:T(1024)} %param.30) | copy-start | bytes 9220
  187.5 40.3 %copy-start.21 = (f32[768]{0:T(1024)S(1)}, f32[768]{0:T(1024)}, u32[]{:S(2)}) copy-start(f32[768]{0:T(1024)} %param.31) | copy-start | bytes 9220
  187.5 73.5 %all-gather.12.cloned.1.call-start = ((), (), s32[]{:S(2)}) async-start(), calls=%async_computation.11 | async-start | bytes 3932160 | tf_op jit(solution)/shard_map/all_gather | solution.py:42
  188.2 41.1 %copy-start.28 = (f32[768]{0:T(1024)S(1)}, f32[768]{0:T(1024)}, u32[]{:S(2)}) copy-start(f32[768]{0:T(1024)} %param.32) | copy-start | bytes 9220
  232.4 84.0 %reduce-scatter.13.cloned.1.call-start = ((), (), s32[]{:S(2)}) async-start(), calls=%async_computation.12 | async-start | bytes 3932160 | tf_op jit(solution)/shard_map/reduce_scatter | solution.py:46
  278.3 72.8 %all-gather.14.cloned.1.call-start = ((), (), s32[]{:S(2)}) async-start(), calls=%async_computation.13 | async-start | bytes 3932160 | tf_op jit(solution)/shard_map/all_gather | solution.py:42
  278.6 6.8 %copy-start.30 = (bf16[2048,768]{1,0:T(8,128)(2,1)S(1)}, bf16[2048,768]{1,0:T(8,128)(2,1)}, u32[]{:S(2)}) copy-start(bf16[2048,768]{1,0:T(8,128)(2,1)} %all-gather.12.cloned.1.call-done) | copy-start | bytes 9437188
  322.5 162.9 %reduce-scatter.17.cloned.1.call-start = ((), (), s32[]{:S(2)}) async-start(), calls=%async_computation.15 | async-start | bytes 2654208 | tf_op jit(solution)/shard_map/reduce_scatter | solution.py:197
  325.8 216.1 %reduce-scatter.19.cloned.1.call-start = ((), (), s32[]{:S(2)}) async-start(), calls=%async_computation.16 | async-start | bytes 1327104
  379.6 5.7 copy-start
  406.5 5.7 copy-start
  476.9 104.4 %reduce-scatter.15.cloned.1.call-start = ((), (), s32[]{:S(2)}) async-start(), calls=%async_computation.14 | async-start | bytes 3932160 | tf_op jit(solution)/shard_map/reduce_scatter | solution.py:46
  483.5 97.8 %copy-start.9 = (f32[512,768]{1,0:T(8,128)S(1)}, f32[512,768]{1,0:T(8,128)}, u32[]{:S(2)}) copy-start(f32[512,768]{1,0:T(8,128)} %get-tuple-element.310) | copy-start | bytes 4718596
  (23 other events, 57.9 us)
Sparse Core Ops, SparseCore 0:
  9.5 31.2 all-gather.5
  43.6 55.7 all-gather.7
  103.3 36.6 reduce-scatter.8
  144.7 28.4 all-gather.9
  187.6 37.8 reduce-scatter.10
  232.5 28.4 all-gather.11
  278.5 37.8 reduce-scatter.12
  322.6 28.4 all-gather.13
  354.7 69.7 reduce-scatter.16
  477.0 64.8 reduce-scatter.18
  544.5 36.7 reduce-scatter.14

commit v2 on v1

--- a/solution.py
+++ b/solution.py
@@ -3,6 +3,8 @@
 import jax
 import jax.numpy as jnp
 from jax import lax
+from jax.experimental import pallas as pl
+from jax.experimental.pallas import tpu as pltpu
 from jax.sharding import PartitionSpec as P
 
 HEAD = 64
@@ -38,12 +40,349 @@
     return lax.dot_general(left, right, (dims, ((), ())), preferred_element_type=F32)
 
 
-def gather_tensor(rows):
-    return lax.all_gather(rows, "tensor", axis=0, tiled=True)
-
-
-def scatter_tensor(part):
-    return lax.psum_scatter(part, "tensor", scatter_dimension=0, tiled=True)
+MESH = pl.DeviceIdType.MESH
+PARTS = 4
+STEPS = 4
+
+
+def remote(src, dst, send, recv, where):
+    return pltpu.make_async_remote_copy(
+        src_ref=src, dst_ref=dst, send_sem=send, recv_sem=recv, device_id=where, device_id_type=MESH
+    )
+
+
+def neighbours():
+    me = lax.axis_index("tensor")
+    partner = me + 1 - 2 * (me % 2)
+    return me, partner, (me + 2) % PARTS, (partner + 2) % PARTS
+
+
+def greet(count, where):
+    barrier = pltpu.get_barrier_semaphore()
+
+    def one(k, carry):
+        pl.semaphore_signal(barrier, inc=1, device_id=where(k), device_id_type=MESH)
+        return carry
+
+    lax.fori_loop(0, count, one, 0)
+    pl.semaphore_wait(barrier, count)
+
+
+def loop(count, body):
+    def step(k, carry):
+        body(k)
+        return carry
+
+    lax.fori_loop(0, count, step, 0)
+
+
+class RowGather:
+    semaphores = [pltpu.SemaphoreType.DMA((2, STEPS))] * 2 + [pltpu.SemaphoreType.DMA((2,))]
+
+    def __init__(self, mine, seq, cross_sems, relay_sems, own_sems):
+        self.mine, self.seq = mine, seq
+        self.cross_sems, self.relay_sems, self.own_sems = cross_sems, relay_sems, own_sems
+        self.me, self.partner, self.cross, self.diag = neighbours()
+        self.rows = mine.shape[0] // STEPS
+
+    def cut(self, k):
+        return pl.ds(pl.multiple_of(k * self.rows, self.rows), self.rows)
+
+    def crossing(self, k):
+        return remote(
+            self.mine.at[self.cut(k)],
+            self.seq.at[self.me, self.cut(k)],
+            self.cross_sems.at[0, k],
+            self.cross_sems.at[1, k],
+            {"tensor": self.cross},
+        )
+
+    def relay(self, k):
+        block = self.seq.at[self.cross, self.cut(k)]
+        return remote(
+            block,
+            block,
+            self.relay_sems.at[0, k],
+            self.relay_sems.at[1, k],
+            {"tensor": self.partner},
+        )
+
+    def own(self):
+        return remote(
+            self.mine,
+            self.seq.at[self.me],
+            self.own_sems.at[0],
+            self.own_sems.at[1],
+            {"tensor": self.partner},
+        )
+
+    def start(self):
+        loop(STEPS, lambda k: self.crossing(k).start())
+        self.own().start()
+        self.seq[self.me] = self.mine[...]
+
+    def finish(self):
+        def arrive(k):
+            self.crossing(k).wait_recv()
+            self.relay(k).start()
+
+        loop(STEPS, arrive)
+        self.own().wait()
+        loop(STEPS, lambda k: self.crossing(k).wait_send())
+        loop(STEPS, lambda k: self.relay(k).wait())
+
+
+def greet_pair():
+    me, partner, cross, diag = neighbours()
+    greet(2, lambda k: {"tensor": partner + k * (cross - partner)})
+
+
+def vmem():
+    return pl.BlockSpec(memory_space=pltpu.VMEM)
+
+
+def gather_kernel(mine, seq, cross_sems, relay_sems, own_sems):
+    greet_pair()
+    rows = RowGather(mine, seq, cross_sems, relay_sems, own_sems)
+    rows.start()
+    rows.finish()
+
+
+def gather_tensor(rows, ident):
+    count, width = rows.shape
+    size = PARTS * count * width * 2
+    seq = pl.pallas_call(
+        gather_kernel,
+        out_shape=jax.ShapeDtypeStruct((PARTS, count, width), rows.dtype),
+        in_specs=[vmem()],
+        out_specs=vmem(),
+        scratch_shapes=RowGather.semaphores,
+        cost_estimate=pl.CostEstimate(flops=0, bytes_accessed=20 * size, transcendentals=0),
+        compiler_params=pltpu.CompilerParams(collective_id=ident, has_side_effects=True),
+        name=f"gather_rows_{ident}",
+    )(rows)
+    return seq.reshape(PARTS * count, width)
+
+
+def start_kernel(tokens, weight, seq, full, cross_sems, relay_sems, own_sems, weight_sems):
+    place, count = lax.axis_index("dp"), lax.axis_size("dp")
+    me, partner, cross, diag = neighbours()
+    barrier = pltpu.get_barrier_semaphore()
+    for where in (partner, cross):
+        pl.semaphore_signal(barrier, inc=1, device_id={"tensor": where}, device_id_type=MESH)
+    loop(
+        count - 1,
+        lambda k: pl.semaphore_signal(
+            barrier, inc=1, device_id={"dp": (place + 1 + k) % count}, device_id_type=MESH
+        ),
+    )
+    pl.semaphore_wait(barrier, count + 1)
+    rows = RowGather(tokens, seq, cross_sems, relay_sems, own_sems)
+
+    def piece(k):
+        return remote(
+            weight,
+            full.at[place],
+            weight_sems.at[0, k],
+            weight_sems.at[1, k],
+            {"dp": (place + 1 + k) % count},
+        )
+
+    loop(count - 1, lambda k: piece(k).start())
+    rows.start()
+    full[place] = weight[...]
+    rows.finish()
+    loop(count - 1, lambda k: piece(k).wait())
+
+
+def start_gather(tokens, weight):
+    count, width = tokens.shape
+    ways = lax.axis_size("dp")
+    seq, full = pl.pallas_call(
+        start_kernel,
+        out_shape=(
+            jax.ShapeDtypeStruct((PARTS, count, width), tokens.dtype),
+            jax.ShapeDtypeStruct((ways,) + weight.shape, weight.dtype),
+        ),
+        in_specs=[vmem()] * 2,
+        out_specs=(vmem(), vmem()),
+        scratch_shapes=RowGather.semaphores + [pltpu.SemaphoreType.DMA((2, ways - 1))],
+        cost_estimate=pl.CostEstimate(flops=0, bytes_accessed=60 << 20, transcendentals=0),
+        compiler_params=pltpu.CompilerParams(collective_id=1, has_side_effects=True),
+        name="start_gather",
+    )(tokens, weight)
+    return seq.reshape(PARTS * count, width), full.reshape(-1, weight.shape[1])
+
+
+class Scatter:
+    def __init__(self, left, weight, out, pair_out, pair_in, over_out, over_in, pair_sems, over_sems):
+        self.left, self.weight, self.out = left, weight, out
+        self.pair_out, self.pair_in = pair_out, pair_in
+        self.over_out, self.over_in = over_out, over_in
+        self.pair_sems, self.over_sems = pair_sems, over_sems
+        self.me, self.partner, self.cross, self.diag = neighbours()
+        self.rows = left.shape[1] // STEPS
+
+    @staticmethod
+    def scratch(rows, width):
+        return [
+            pltpu.VMEM((2, rows, width), BF16),
+            pltpu.VMEM((2, rows, width), BF16),
+            pltpu.VMEM((rows, width), BF16),
+            pltpu.VMEM((rows, width), BF16),
+            pltpu.SemaphoreType.DMA((2, 2, STEPS)),
+            pltpu.SemaphoreType.DMA((2, STEPS)),
+        ]
+
+    def cut(self, k):
+        return pl.ds(pl.multiple_of(k * self.rows, self.rows), self.rows)
+
+    def pair(self, which, k):
+        return remote(
+            self.pair_out.at[which, self.cut(k)],
+            self.pair_in.at[which, self.cut(k)],
+            self.pair_sems.at[0, which, k],
+            self.pair_sems.at[1, which, k],
+            {"tensor": self.partner},
+        )
+
+    def over(self, k):
+        return remote(
+            self.over_out.at[self.cut(k)],
+            self.over_in.at[self.cut(k)],
+            self.over_sems.at[0, k],
+            self.over_sems.at[1, k],
+            {"tensor": self.cross},
+        )
+
+    def product(self, block, k):
+        return mm(self.left[block, self.cut(k)], self.weight[...], ((1,), (1,)))
+
+    def run(self):
+        def away(which, block):
+            def body(k):
+                self.pair_out[which, self.cut(k)] = self.product(block, k).astype(BF16)
+                self.pair(which, k).start()
+
+            return body
+
+        def across(k):
+            part = self.product(self.cross, k)
+            self.pair(0, k).wait_recv()
+            part = part + self.pair_in[0, self.cut(k)].astype(F32)
+            self.over_out[self.cut(k)] = part.astype(BF16)
+            self.over(k).start()
+
+        def home(k):
+            part = self.product(self.me, k)
+            self.pair(1, k).wait_recv()
+            self.out[self.cut(k)] = part + self.pair_in[1, self.cut(k)].astype(F32)
+
+        def close(k):
+            self.over(k).wait_recv()
+            self.out[self.cut(k)] = self.out[self.cut(k)] + self.over_in[self.cut(k)].astype(F32)
+
+        loop(STEPS, away(0, self.diag))
+        loop(STEPS, across)
+        loop(STEPS, away(1, self.partner))
+        loop(STEPS, home)
+        loop(STEPS, close)
+        for which in range(2):
+            loop(STEPS, lambda k: self.pair(which, k).wait_send())
+        loop(STEPS, lambda k: self.over(k).wait_send())
+
+
+def scatter_kernel(left, weight, out, *scratch):
+    greet_pair()
+    Scatter(left, weight, out, *scratch).run()
+
+
+def scatter_tensor(left, weight, ident):
+    rows, inner = left.shape[0] // PARTS, left.shape[1]
+    width = weight.shape[0]
+    return pl.pallas_call(
+        scatter_kernel,
+        out_shape=jax.ShapeDtypeStruct((rows, width), F32),
+        in_specs=[vmem()] * 2,
+        out_specs=vmem(),
+        scratch_shapes=Scatter.scratch(rows, width),
+        cost_estimate=pl.CostEstimate(
+            flops=2 * PARTS * rows * inner * width, bytes_accessed=60 << 20, transcendentals=0
+        ),
+        compiler_params=pltpu.CompilerParams(collective_id=ident, has_side_effects=True),
+        name=f"scatter_rows_{ident}",
+    )(left.reshape(PARTS, rows, inner), weight)
+
+
+def tail_kernel(left, weight, grads, small, out, grads_out, small_out, *scratch):
+    scatter_scratch, (grads_in, small_in, grad_sems, small_sems) = scratch[:6], scratch[6:]
+    place, count = lax.axis_index("dp"), lax.axis_size("dp")
+    me = place * PARTS + lax.axis_index("tensor")
+    ways = count * PARTS
+
+    def rank(k):
+        peer = (me + 1 + k) % ways
+        return {"dp": peer // PARTS, "tensor": peer % PARTS}
+
+    greet(ways - 1, rank)
+
+    def grad(k):
+        peer = (place + 1 + k) % count
+        return remote(
+            grads.at[peer], grads_in.at[k], grad_sems.at[0, k], grad_sems.at[1, k], {"dp": peer}
+        )
+
+    def bit(k):
+        peer = (me + 1 + k) % ways
+        return remote(
+            small.at[peer], small_in.at[k], small_sems.at[0, k], small_sems.at[1, k], rank(k)
+        )
+
+    loop(count - 1, lambda k: grad(k).start())
+    loop(ways - 1, lambda k: bit(k).start())
+    Scatter(left, weight, out, *scatter_scratch).run()
+    small_out[...] = small[me]
+
+    def add_bit(k):
+        bit(k).wait()
+        small_out[...] = small_out[...] + small_in[k]
+
+    loop(ways - 1, add_bit)
+    grads_out[...] = grads[place].astype(F32)
+
+    def add_grad(k):
+        grad(k).wait()
+        grads_out[...] = grads_out[...] + grads_in[k].astype(F32)
+
+    loop(count - 1, add_grad)
+
+
+def tail(left, weight, grads, small):
+    rows, inner = left.shape[0] // PARTS, left.shape[1]
+    width = weight.shape[0]
+    count, ways = grads.shape[0], small.shape[0]
+    return pl.pallas_call(
+        tail_kernel,
+        out_shape=(
+            jax.ShapeDtypeStruct((rows, width), F32),
+            jax.ShapeDtypeStruct(grads.shape[1:], F32),
+            jax.ShapeDtypeStruct(small.shape[1:], F32),
+        ),
+        in_specs=[vmem()] * 4,
+        out_specs=(vmem(),) * 3,
+        scratch_shapes=Scatter.scratch(rows, width)
+        + [
+            pltpu.VMEM((count - 1,) + grads.shape[1:], BF16),
+            pltpu.VMEM((ways - 1,) + small.shape[1:], F32),
+            pltpu.SemaphoreType.DMA((2, count - 1)),
+            pltpu.SemaphoreType.DMA((2, ways - 1)),
+        ],
+        cost_estimate=pl.CostEstimate(
+            flops=2 * PARTS * rows * inner * width, bytes_accessed=90 << 20, transcendentals=0
+        ),
+        compiler_params=pltpu.CompilerParams(collective_id=9, has_side_effects=True),
+        name="tail",
+    )(left.reshape(PARTS, rows, inner), weight, grads, small)
 
 
 def attention_forward(queries, key_rows, value_rows, length):
@@ -145,13 +484,12 @@
     depth = up_weight.shape[0]
     length = lengths[0]
     qkv_rows = jnp.concatenate([qkv_weight[0], qkv_weight[1], qkv_weight[2]], axis=1)
-    qkv_full = lax.all_gather(qkv_rows, "dp", axis=0, tiled=True)
+    seq_tokens, qkv_full = start_gather(tokens, qkv_rows)
     rest_rows = jnp.concatenate([up_weight, down_weight.T, out_weight.T], axis=1)
     rest_full = lax.all_gather(rest_rows, "dp", axis=0, tiled=True)
     up_full = rest_full[:, :unit_cols]
     down_full = rest_full[:, unit_cols : 2 * unit_cols]
     out_full = rest_full[:, 2 * unit_cols :]
-    seq_tokens = gather_tensor(tokens)
     row_start = piece * local_rows
     row_valid = row_start + jnp.arange(local_rows, dtype=jnp.int32) < length
     head_start = piece * head_cols
@@ -163,15 +501,15 @@
     key_rows = projected[:, head_cols : 2 * head_cols]
     value_rows = projected[:, 2 * head_cols :]
     mixed, log_totals = attention_forward(queries, key_rows, value_rows, length)
-    attn_local = scatter_tensor(mm(mixed, out_full, ((1,), (1,))).astype(BF16)).astype(F32)
+    attn_local = scatter_tensor(mixed, out_full, 2)
     first_out, first_normed, first_inverse = norm_rows(
         tokens.astype(F32) + (attn_local + out_bias), first_gain, first_shift
     )
-    seq_first = gather_tensor(first_out.astype(BF16))
+    seq_first = gather_tensor(first_out.astype(BF16), 3)
     up_cols = lax.dynamic_slice_in_dim(up_bias, unit_start, unit_cols, 0)
     pre_act = mm(seq_first, up_full, ((1,), (0,))) + up_cols
     activated = gelu_tanh(pre_act).astype(BF16)
-    ffn_local = scatter_tensor(mm(activated, down_full, ((1,), (1,))).astype(BF16)).astype(F32)
+    ffn_local = scatter_tensor(activated, down_full, 4)
     second_in = first_out + (ffn_local + down_bias)
     layer_out, second_normed, second_inverse = norm_rows(second_in, second_gain, second_shift)
     upstream = cotangent.astype(F32) * row_valid[:, None].astype(F32)
@@ -181,10 +519,10 @@
     ffn_grad = grad_second.astype(BF16)
     down_bias_part = jnp.sum(ffn_grad.astype(F32), axis=0)
     unused_value, gelu_pull = jax.vjp(gelu_tanh, pre_act)
-    seq_ffn_grad = gather_tensor(ffn_grad)
+    seq_ffn_grad = gather_tensor(ffn_grad, 5)
     act_grad = mm(seq_ffn_grad, down_full, ((1,), (0,)))
     pre_grad = gelu_pull(act_grad)[0].astype(BF16)
-    first_back = scatter_tensor(mm(pre_grad, up_full, ((1,), (1,))).astype(BF16)).astype(F32)
+    first_back = scatter_tensor(pre_grad, up_full, 6)
     up_bias_part = jnp.sum(pre_grad.astype(F32), axis=0)
     down_grad = mm(seq_ffn_grad, activated, ((0,), (0,))).astype(BF16)
     up_grad = mm(seq_first, pre_grad, ((0,), (0,))).astype(BF16)
@@ -197,19 +535,14 @@
     grad_ud = lax.psum_scatter(
         jnp.concatenate([up_grad, down_grad], axis=1), "dp", scatter_dimension=0, tiled=True
     )
-    seq_attn_grad = gather_tensor(attn_grad)
+    seq_attn_grad = gather_tensor(attn_grad, 7)
     out_grad = mm(seq_attn_grad, mixed, ((0,), (0,))).astype(BF16)
     mixed_grad = mm(seq_attn_grad, out_full, ((1,), (0,))).astype(BF16)
     query_grad, key_grad, value_grad = attention_backward(
         queries, key_rows, value_rows, mixed_grad, log_totals, length
     )
     stacked = jnp.concatenate([query_grad, key_grad, value_grad], axis=1)
-    token_back = scatter_tensor(mm(stacked, qkv_full, ((1,), (1,))).astype(BF16)).astype(F32)
     qkv_grad = mm(seq_tokens, stacked, ((0,), (0,))).astype(BF16)
-    grad_qo = lax.psum_scatter(
-        jnp.concatenate([qkv_grad, out_grad], axis=1), "dp", scatter_dimension=0, tiled=True
-    )
-    grad_tokens = grad_first + token_back
     zeros_heads = jnp.zeros((width,), F32)
     query_bias = lax.dynamic_update_slice(
         zeros_heads, jnp.sum(query_grad.astype(F32), axis=0), (head_start,)
@@ -237,14 +570,19 @@
         ],
         axis=1,
     )
-    small = lax.psum_scatter(small, ("dp", "tensor"), scatter_dimension=0, tiled=True)[0]
+    bits_wide = small.shape[1]
+    padded = -(-bits_wide // 1024) * 1024
+    small = jnp.pad(small, ((0, 0), (0, padded - bits_wide))).reshape(ways, -1, 128)
+    grads = jnp.concatenate([qkv_grad, out_grad], axis=1).reshape(-1, depth, 4 * head_cols)
+    token_back, grad_qo, small = tail(stacked, qkv_full, grads, small)
+    small = small.reshape(-1)
+    grad_tokens = grad_first + token_back
     share = width // ways
     cuts = [0]
     for size in (share, share, share, share, share, up_bias.shape[0] // ways, share, share, share):
         cuts.append(cuts[-1] + size)
     bits = [small[cuts[i] : cuts[i + 1]] for i in range(9)]
     grad_ud = grad_ud.astype(F32)
-    grad_qo = grad_qo.astype(F32)
     grad_qkv = jnp.stack([grad_qo[:, i * head_cols : (i + 1) * head_cols] for i in range(3)])
     return (
         layer_out.astype(BF16),

time: 600 us -> 524 us (0.87)
  Pallas kernels: 0 us -> 239 us
  waiting for transfers between devices: 237 us -> 0.04 us
  blocking collectives: 74.5 us -> 0 us
  matrix products: 169 us -> 149 us
  local copies, waits for them, and re-layouts: 27.9 us -> 44 us
    pallas_call x0 -> x8, Pallas kernels: none -> 239 us  [the longest x3 88.5 us: scatter_tensor(): pl.pallas_call(scatter_kernel, out_shape=jax.ShapeDtypeStruct((rows, widt...]
    reduce_scatter x4 -> x0, waiting for transfers between devices: 134 us -> none  [scatter_tensor(): return lax.psum_scatter(part, 'tensor', scatter_dimension=0, tiled=True)]
    all_gather x4 -> x0, waiting for transfers between devices: 81.1 us -> none  [gather_tensor(): return lax.all_gather(rows, 'tensor', axis=0, tiled=True)]
    unnamed x1 -> x0, blocking collectives: 39.8 us -> none
    all_gather x1 -> x0, blocking collectives: 34.7 us -> none  [per_device(): qkv_full = lax.all_gather(qkv_rows, 'dp', axis=0, tiled=True)]
    dot_general x12 -> x8, matrix products: 62.3 us -> 41.7 us  [mm(): lax.dot_general(left, right, (dims, ((), ())), preferred_element_type=F32)]
    unnamed x12 -> x2, waiting for transfers between devices: 12.4 us -> 0.03 us
    all_gather x1, waiting for transfers between devices: 9.14 us -> 0.01 us  [per_device(): rest_full = lax.all_gather(rest_rows, 'dp', axis=0, tiled=True)]
  transfers between devices with their start and end apart: 11 -> 2, of which waited for: 9 -> 0; matrix products, arithmetic and copies ran while one was open for 35% -> 37% of each run, Pallas kernels for 0% -> 16%
where the time goes in v2:
time: 524 us; the launch traced here: 519 us
  Pallas kernels  239 us (46%)
  matrix products  149 us (28%)
  other arithmetic  70.7 us (13%)
  local copies, waits for them, and re-layouts  44 us (8%)
  between operations  15.5 us (3%)
    pallas_call x3, Pallas kernels, scatter_tensor(): pl.pallas_call(scatter_kernel, out_shape=jax.ShapeDtypeStruct((rows, widt...  88.5 us
    pallas_call x3, Pallas kernels, gather_tensor(): pl.pallas_call(gather_kernel, out_shape=jax.ShapeDtypeStruct((PARTS, coun...  70.2 us
    pallas_call x1, Pallas kernels, tail(): pl.pallas_call(tail_kernel, out_shape=(jax.ShapeDtypeStruct((rows, width)...  44.4 us
    dot_general x8, matrix products, mm(): lax.dot_general(left, right, (dims, ((), ())), preferred_element_type=F32)  41.7 us
    pallas_call x1, Pallas kernels, start_gather(): pl.pallas_call(start_kernel, out_shape=(jax.ShapeDtypeStruct((PARTS, coun...  36.3 us
    dot_general x4, matrix products, back_block(): jnp.einsum('hqk,khd->qhd', score_grad, key_heads, preferred_element_type=...  22.7 us
    dot_general x4, matrix products, back_block(): jnp.einsum('hqk,qhd->khd', probs.astype(BF16), grad_block, preferred_elem...  21.6 us
    convert_element_type x4, other arithmetic, back_block(): score_grad = (probs * (prob_grad - centre)).astype(BF16)  19.9 us
  transfers between devices with their start and end apart: 2, of which 0 were waited for; matrix products, arithmetic and copies ran while one was open for 37% of the time, Pallas kernels for 16%

profile of v2, /device:TPU:0, one launch (start us, length us, event | category | flops | bytes accessed | tf_op | source)
XLA Modules:
  0.0 519.1 jit_solution(4805134599699143292)
XLA Ops:
  11.6 36.3 %start_gather.1 = (bf16[4,512,768]{2,1,0:T(8,128)(2,1)}, bf16[8,96,576]{2,1,0:T(8,128)(2,1)}) custom-call(bf16[512,768]{1,0:T(8,128)(2,1)} %tokens.1, bf16[96,576]{1,0:T(8,128)(2,1)} %pad_maximum_fusion.5.weight), custom_call_target="tpu_custom_call" | custom-call | bytes 62914560 | tf_op jit(solution)/shard_map/start_gather/pallas_call | solution.py:201
  54.1 36.8 %while.28 = (s32[]{:T(128)}, bf16[4,512,3,64]{1,3,2,0:T(8,128)(2,1)S(1)}, f32[4,3,512]{2,1,0:T(4,128)S(1)}, bf16[4,512,3,64]{1,3,2,0:T(8,128)(2,1)S(1)}, bf16[20...) while((s32[]{:T(128)}, ...), condition=%wide.region_3.4_spmd.clone, body=%wide.region_0.3_spmd.clone.sunk | while | flops 843153920 | bytes 39782508 | solution.py:411
  99.6 24.5 %scatter_rows_2.1 = f32[512,768]{1,0:T(8,128)} custom-call(bf16[4,512,192]{2,1,0:T(8,128)(2,1)} %copy.41.left, bf16[768,192]{1,0:T(8,128)(2,1)} %slice.107.weight), custom_call_target="tpu_custom_call" | custom-call | flops 603979776 | bytes 62914560 | tf_op jit(solution)/shard_map/scatter_rows_2/pallas_call | solution.py:303
  128.4 23.7 %gather_rows_3.1 = bf16[4,512,768]{2,1,0:T(8,128)(2,1)} custom-call(bf16[512,768]{1,0:T(8,128)(2,1)} %fusion.67.mine), custom_call_target="tpu_custom_call" | custom-call | bytes 62914560 | tf_op jit(solution)/shard_map/gather_rows_3/pallas_call | solution.py:154
  155.4 7.1 %fusion.54 = (bf16[2048,768]{1,0:T(8,128)(2,1)}, f32[2048,768]{1,0:T(8,128)}) fusion(f32[768]{0:T(1024)S(1)} %dynamic_slice.21, bf16[2048,768]{1,0:T(8,128)(2,1)S(1)} %bitcast.169, bf16[768,1728]{1,0:T(8,128)(2,1)} %all-gather.2.cloned.1.call-done), kind=kOutput, calls=%fused_computation.64 | convolution fusion | flops 2431647744 | bytes 13765632 | tf_op jit(solution)/shard_map/dot_general | solution.py:40
  162.5 37.7 %scatter_rows_4.1 = f32[512,768]{1,0:T(8,128)} custom-call(bf16[4,512,768]{2,1,0:T(8,128)(2,1)} %bitcast.186, bf16[768,768]{1,0:T(8,128)(2,1)} %get-tuple-element.301.weight), custom_call_target="tpu_custom_call" | custom-call | flops 2415919104 | bytes 62914560 | tf_op jit(solution)/shard_map/scatter_rows_4/pallas_call | solution.py:303
  206.7 23.4 %gather_rows_5.1 = bf16[4,512,768]{2,1,0:T(8,128)(2,1)} custom-call(bf16[512,768]{1,0:T(8,128)(2,1)} %get-tuple-element.285.mine), custom_call_target="tpu_custom_call" | custom-call | bytes 62914560 | tf_op jit(solution)/shard_map/gather_rows_5/pallas_call | solution.py:154
  230.1 6.8 %convolution_convert_fusion.1 = bf16[768,768]{1,0:T(8,128)(2,1)} fusion(bf16[2048,768]{1,0:T(8,128)(2,1)} %bitcast.171, bf16[2048,768]{1,0:T(8,128)(2,1)} %get-tuple-element.323), kind=kOutput, calls=%fused_computation.95 | convolution fusion | flops 2416508928 | bytes 7471104 | tf_op jit(solution)/shard_map/dot_general | solution.py:40
  236.9 9.9 %convert_reduce_fusion = (f32[768]{0:T(1024)}, bf16[2048,768]{1,0:T(8,128)(2,1)S(1)}) fusion(f32[2048,768]{1,0:T(8,128)} %get-tuple-element.324, f32[768]{0:T(1024)S(1)} %dynamic_slice.21, bf16[2048,768]{1,0:T(8,128)(2,1)S(1)} %bitcast.172, bf16[768,1728]{1,0:T(8,128)(2,1)} %all-gather.2.cloned.1.call-done), kind=kOutput, calls=%fused_computation.62 | convolution fusion | flops 2458385664 | bytes 13768704 | tf_op jit(solution)/shard_map/dot_general | solution.py:40
  250.5 26.3 %scatter_rows_6.1 = f32[512,768]{1,0:T(8,128)} custom-call(bf16[4,512,768]{2,1,0:T(8,128)(2,1)} %bitcast.187, bf16[768,768]{1,0:T(8,128)(2,1)} %get-tuple-element.300.weight), custom_call_target="tpu_custom_call" | custom-call | flops 2415919104 | bytes 62914560 | tf_op jit(solution)/shard_map/scatter_rows_6/pallas_call | solution.py:303
  284.1 23.0 %gather_rows_7.1 = bf16[4,512,768]{2,1,0:T(8,128)(2,1)} custom-call(bf16[512,768]{1,0:T(8,128)(2,1)} %get-tuple-element.118.mine), custom_call_target="tpu_custom_call" | custom-call | bytes 62914560 | tf_op jit(solution)/shard_map/gather_rows_7/pallas_call | solution.py:154
  320.6 107.3 %while.29 = (s32[]{:T(128)}, f32[2048,3,64]{0,2,1:T(8,128)S(1)}, f32[2048,3,64]{0,2,1:T(8,128)}, bf16[4,512,3,64]{1,3,2,0:T(8,128)(2,1)}, bf16[4,512,3,64]{1,3,2...) while((s32[]{:T(128)}, f32[2048,3,64]{0,2,1:T(8,128)S(1)}, ...), condition=%wide.region_14.15_spmd.clone, body=%wide.region_12.14_spmd.clone.sunk | while | flops 2062615040 | bytes 129222840 | solution.py:452
  334.2 5.0 multiply_convert_fusion.2
  339.2 5.7 %fusion.140 = bf16[4,512,3,64]{1,3,2,0:T(8,128)(2,1)} fusion(bf16[4,512,3,64]{1,3,2,0:T(8,128)(2,1)} %get-tuple-element.480, s32[]{:T(128)S(6)} %copy.70, bf16[3,512,2048]{2,1,0:T(8,128)(2,1)} %multiply_convert_fusion.2, bf16[2048,3,64]{0,2,1:T(8,128)(2,1)S(1)} %get-tuple-element.494), kind=kOutput, calls=%fused_computation.33.clone.1 | convolution fusion | flops 402849792 | bytes 7274500 | tf_op jit(solution)/shard_map/while/body/eval_jaxpr/hqk,khd->qhd/dot_general | solution.py:442
  350.7 5.6 %fusion.139 = f32[2048,3,64]{0,2,1:T(8,128)} fusion(f32[3,512,2048]{2,1,0:T(8,128)S(1)} %fusion.137, f32[3,512]{1,0:T(4,128)S(1)} %dynamic-slice_bitcast_fusion.2, pred[2048]{0:T(1024)(128)(4,1)S(1)} %iota_compare_fusion.5, f32[2048,3,64]{0,2,1:T(8,128)} %get-tuple-element.479, pred[]{:T(512)S(6)} %compare.4, ...), kind=kOutput, calls=%fused_computation.29.clone.1 | convolution fusion | flops 416022528 | bytes 15933445 | tf_op jit(solution)/shard_map/while/body/eval_jaxpr/hqk,qhd->khd/dot_general | solution.py:435
  361.1 5.0 multiply_convert_fusion.2
  366.1 5.7 %fusion.140 = bf16[4,512,3,64]{1,3,2,0:T(8,128)(2,1)} fusion(bf16[4,512,3,64]{1,3,2,0:T(8,128)(2,1)} %get-tuple-element.480, s32[]{:T(128)S(6)} %copy.70, bf16[3,512,2048]{2,1,0:T(8,128)(2,1)} %multiply_convert_fusion.2, bf16[2048,3,64]{0,2,1:T(8,128)(2,1)S(1)} %get-tuple-element.494), kind=kOutput, calls=%fused_computation.33.clone.1 | convolution fusion | flops 402849792 | bytes 7274500 | tf_op jit(solution)/shard_map/while/body/eval_jaxpr/hqk,khd->qhd/dot_general | solution.py:442
  377.6 5.5 %fusion.139 = f32[2048,3,64]{0,2,1:T(8,128)} fusion(f32[3,512,2048]{2,1,0:T(8,128)S(1)} %fusion.137, f32[3,512]{1,0:T(4,128)S(1)} %dynamic-slice_bitcast_fusion.2, pred[2048]{0:T(1024)(128)(4,1)S(1)} %iota_compare_fusion.5, f32[2048,3,64]{0,2,1:T(8,128)} %get-tuple-element.479, pred[]{:T(512)S(6)} %compare.4, ...), kind=kOutput, calls=%fused_computation.29.clone.1 | convolution fusion | flops 416022528 | bytes 15933445 | tf_op jit(solution)/shard_map/while/body/eval_jaxpr/hqk,qhd->khd/dot_general | solution.py:435
  388.0 5.0 multiply_convert_fusion.2
  393.0 5.7 %fusion.140 = bf16[4,512,3,64]{1,3,2,0:T(8,128)(2,1)} fusion(bf16[4,512,3,64]{1,3,2,0:T(8,128)(2,1)} %get-tuple-element.480, s32[]{:T(128)S(6)} %copy.70, bf16[3,512,2048]{2,1,0:T(8,128)(2,1)} %multiply_convert_fusion.2, bf16[2048,3,64]{0,2,1:T(8,128)(2,1)S(1)} %get-tuple-element.494), kind=kOutput, calls=%fused_computation.33.clone.1 | convolution fusion | flops 402849792 | bytes 7274500 | tf_op jit(solution)/shard_map/while/body/eval_jaxpr/hqk,khd->qhd/dot_general | solution.py:442
  404.5 5.5 %fusion.139 = f32[2048,3,64]{0,2,1:T(8,128)} fusion(f32[3,512,2048]{2,1,0:T(8,128)S(1)} %fusion.137, f32[3,512]{1,0:T(4,128)S(1)} %dynamic-slice_bitcast_fusion.2, pred[2048]{0:T(1024)(128)(4,1)S(1)} %iota_compare_fusion.5, f32[2048,3,64]{0,2,1:T(8,128)} %get-tuple-element.479, pred[]{:T(512)S(6)} %compare.4, ...), kind=kOutput, calls=%fused_computation.29.clone.1 | convolution fusion | flops 416022528 | bytes 15933445 | tf_op jit(solution)/shard_map/while/body/eval_jaxpr/hqk,qhd->khd/dot_general | solution.py:435
  414.9 5.0 multiply_convert_fusion.2
  419.8 5.6 %fusion.140 = bf16[4,512,3,64]{1,3,2,0:T(8,128)(2,1)} fusion(bf16[4,512,3,64]{1,3,2,0:T(8,128)(2,1)} %get-tuple-element.480, s32[]{:T(128)S(6)} %copy.70, bf16[3,512,2048]{2,1,0:T(8,128)(2,1)} %multiply_convert_fusion.2, bf16[2048,3,64]{0,2,1:T(8,128)(2,1)S(1)} %get-tuple-element.494), kind=kOutput, calls=%fused_computation.33.clone.1 | convolution fusion | flops 402849792 | bytes 7274500 | tf_op jit(solution)/shard_map/while/body/eval_jaxpr/hqk,khd->qhd/dot_general | solution.py:442
  456.4 44.4 %tail.1 = (f32[512,768]{1,0:T(8,128)}, f32[96,768]{1,0:T(8,128)}, f32[8,128]{1,0:T(8,128)}) custom-call(bf16[4,512,576]{2,1,0:T(8,128)(2,1)} %pad_maximum_fusion.left, bf16[768,576]{1,0:T(8,128)(2,1)} %bitcast.185, bf16[8,96,768]{2,1,0:T(8,128)(2,1)} %bitcast.173, f32[32,8,128]{2,1,0:T(8,128)} %bitcast.177), custom_call_target="tpu_custom_call" | custom-call | flops 1811939328 | bytes 94371840 | tf_op jit(solution)/shard_map/tail/pallas_call | solution.py:364
  (210 shorter events, 180.4 us)
Async XLA Ops:
  7.2 90.6 %all-gather.2.cloned.1.call-start = ((), (), s32[]{:S(2)}) async-start(), calls=%async_computation.1 | async-start | bytes 3096576 | tf_op jit(solution)/shard_map/all_gather | solution.py:489
  9.9 498.8 %reduce-scatter.2.cloned.1.call-start = ((), (), s32[]{:S(2)}) async-start(), calls=%async_computation.2 | async-start | bytes 2654208 | tf_op jit(solution)/shard_map/reduce_scatter | solution.py:535
  94.8 29.3 %copy-start.31 = (f32[768]{0:T(1024)S(1)}, f32[768]{0:T(1024)}, u32[]{:S(2)}) copy-start(f32[768]{0:T(1024)} %param.24) | copy-start | bytes 9220
  162.5 37.7 %copy-start.32 = (f32[768]{0:T(1024)S(1)}, f32[768]{0:T(1024)}, u32[]{:S(2)}) copy-start(f32[768]{0:T(1024)} %param.30) | copy-start | bytes 9220
  230.1 6.8 %copy-start.17 = (bf16[4,512,768]{2,1,0:T(8,128)(2,1)S(1)}, bf16[4,512,768]{2,1,0:T(8,128)(2,1)}, u32[]{:S(2)}) copy-start(bf16[4,512,768]{2,1,0:T(8,128)(2,1)} %gather_rows_5.1) | copy-start | bytes 9437188
  236.9 9.9 %copy-start.16 = (bf16[4,512,768]{2,1,0:T(8,128)(2,1)S(1)}, bf16[4,512,768]{2,1,0:T(8,128)(2,1)}, u32[]{:S(2)}) copy-start(bf16[4,512,768]{2,1,0:T(8,128)(2,1)} %gather_rows_3.1) | copy-start | bytes 9437188
  250.5 26.3 %copy-start.28 = (f32[768]{0:T(1024)S(1)}, f32[768]{0:T(1024)}, u32[]{:S(2)}) copy-start(f32[768]{0:T(1024)} %param.32) | copy-start | bytes 9220
  276.8 4.7 copy-start.2
  320.5 107.3 %copy-start.22 = (f32[768]{0:T(1024)S(1)}, f32[768]{0:T(1024)}, u32[]{:S(2)}) copy-start(f32[768]{0:T(1024)} %get-tuple-element.244) | copy-start | bytes 9220
  320.5 107.4 %copy-start.21 = (f32[768]{0:T(1024)S(1)}, f32[768]{0:T(1024)}, u32[]{:S(2)}) copy-start(f32[768]{0:T(1024)} %get-tuple-element.249) | copy-start | bytes 9220
  320.5 107.5 %copy-start.23 = (f32[768]{0:T(1024)S(1)}, f32[768]{0:T(1024)}, u32[]{:S(2)}) copy-start(f32[768]{0:T(1024)} %get-tuple-element.284) | copy-start | bytes 9220
  320.5 107.6 %copy-start.29 = (f32[768]{0:T(1024)S(1)}, f32[768]{0:T(1024)}, u32[]{:S(2)}) copy-start(f32[768]{0:T(1024)} %get-tuple-element.325) | copy-start | bytes 9220
  320.5 108.0 %copy-start.27 = (f32[768]{0:T(1024)S(1)}, f32[768]{0:T(1024)}, u32[]{:S(2)}) copy-start(f32[768]{0:T(1024)} %get-tuple-element.286) | copy-start | bytes 9220
  320.5 108.1 %copy-start.25 = (f32[768]{0:T(1024)S(1)}, f32[768]{0:T(1024)}, u32[]{:S(2)}) copy-start(f32[768]{0:T(1024)} %get-tuple-element.242) | copy-start | bytes 9220
  320.5 108.2 %copy-start.24 = (f32[768]{0:T(1024)S(1)}, f32[768]{0:T(1024)}, u32[]{:S(2)}) copy-start(f32[768]{0:T(1024)} %get-tuple-element.247) | copy-start | bytes 9220
  339.2 5.7 %copy-start = (bf16[3,512,2048]{2,1,0:T(8,128)(2,1)S(1)}, bf16[3,512,2048]{2,1,0:T(8,128)(2,1)}, u32[]{:S(2)}) copy-start(bf16[3,512,2048]{2,1,0:T(8,128)(2,1)} %multiply_convert_fusion.2) | copy-start | bytes 18874372 | tf_op jit(solution)/shard_map/while
  366.1 5.7 %copy-start = (bf16[3,512,2048]{2,1,0:T(8,128)(2,1)S(1)}, bf16[3,512,2048]{2,1,0:T(8,128)(2,1)}, u32[]{:S(2)}) copy-start(bf16[3,512,2048]{2,1,0:T(8,128)(2,1)} %multiply_convert_fusion.2) | copy-start | bytes 18874372 | tf_op jit(solution)/shard_map/while
  393.0 5.7 %copy-start = (bf16[3,512,2048]{2,1,0:T(8,128)(2,1)S(1)}, bf16[3,512,2048]{2,1,0:T(8,128)(2,1)}, u32[]{:S(2)}) copy-start(bf16[3,512,2048]{2,1,0:T(8,128)(2,1)} %multiply_convert_fusion.2) | copy-start | bytes 18874372 | tf_op jit(solution)/shard_map/while
  419.8 5.6 %copy-start = (bf16[3,512,2048]{2,1,0:T(8,128)(2,1)S(1)}, bf16[3,512,2048]{2,1,0:T(8,128)(2,1)}, u32[]{:S(2)}) copy-start(bf16[3,512,2048]{2,1,0:T(8,128)(2,1)} %multiply_convert_fusion.2) | copy-start | bytes 18874372 | tf_op jit(solution)/shard_map/while
  428.9 4.2 copy-start.12
  433.2 8.0 %copy-start.4 = (bf16[4,512,768]{2,1,0:T(8,128)(2,1)S(1)}, bf16[4,512,768]{2,1,0:T(8,128)(2,1)}, u32[]{:S(2)}) copy-start(bf16[4,512,768]{2,1,0:T(8,128)(2,1)} %gather_rows_7.1) | copy-start | bytes 9437188
  447.3 4.1 copy-start.7
  456.4 47.6 %copy-start.10 = (f32[512,768]{1,0:T(8,128)S(1)}, f32[512,768]{1,0:T(8,128)}, u32[]{:S(2)}) copy-start(f32[512,768]{1,0:T(8,128)} %get-tuple-element.288) | copy-start | bytes 4718596
  502.1 4.7 copy-start.30
  (15 other events, 37.3 us)
Sparse Core Ops, SparseCore 0:
  10.2 73.3 all-gather.1
  319.7 75.4 reduce-scatter.1

commit v3 on v2

--- a/solution.py
+++ b/solution.py
@@ -385,78 +385,207 @@
     )(left.reshape(PARTS, rows, inner), weight, grads, small)
 
 
-def attention_forward(queries, key_rows, value_rows, length):
-    total_rows, head_cols = queries.shape
-    head_count = head_cols // HEAD
-    scale = 1.0 / math.sqrt(HEAD)
-    block = min(512, total_rows)
-    blocks = total_rows // block
-    key_valid = jnp.arange(total_rows, dtype=jnp.int32) < length
-    key_heads = key_rows.reshape(total_rows, head_count, HEAD)
-    value_heads = value_rows.reshape(total_rows, head_count, HEAD)
-    query_blocks = queries.reshape(blocks, block, head_count, HEAD)
-
-    def attend_block(query_block):
-        scores = (
-            jnp.einsum("qhd,khd->hqk", query_block, key_heads, preferred_element_type=F32) * scale
-        )
-        scores = jnp.where(key_valid[None, None, :], scores, NEGATIVE)
-        top_score = jnp.max(scores, axis=-1, keepdims=True)
-        expo = jnp.exp(scores - top_score)
-        row_total = jnp.sum(expo, axis=-1, keepdims=True)
-        probs = (expo / row_total).astype(BF16)
-        context = jnp.einsum("hqk,khd->qhd", probs, value_heads, preferred_element_type=F32)
-        return (context.astype(BF16), (top_score + jnp.log(row_total))[..., 0])
-
-    context_blocks, log_totals = lax.map(attend_block, query_blocks)
-    return context_blocks.reshape(total_rows, head_cols), log_totals
-
-
-def attention_backward(queries, key_rows, value_rows, mixed_grad, log_totals, length):
-    total_rows, head_cols = queries.shape
-    head_count = head_cols // HEAD
-    scale = 1.0 / math.sqrt(HEAD)
-    block = min(512, total_rows)
-    blocks = total_rows // block
-    key_valid = jnp.arange(total_rows, dtype=jnp.int32) < length
-    key_heads = key_rows.reshape(total_rows, head_count, HEAD)
-    value_heads = value_rows.reshape(total_rows, head_count, HEAD)
-    query_blocks = queries.reshape(blocks, block, head_count, HEAD)
-    mixed_blocks = mixed_grad.reshape(blocks, block, head_count, HEAD)
-
-    def back_block(carry, inputs):
-        key_acc, value_acc = carry
-        query_block, grad_block, log_total = inputs
-        scores = (
-            jnp.einsum("qhd,khd->hqk", query_block, key_heads, preferred_element_type=F32) * scale
-        )
-        scores = jnp.where(key_valid[None, None, :], scores, NEGATIVE)
-        probs = jnp.exp(scores - log_total[:, :, None])
-        value_acc = value_acc + jnp.einsum(
-            "hqk,qhd->khd", probs.astype(BF16), grad_block, preferred_element_type=F32
-        )
-        prob_grad = jnp.einsum("qhd,khd->hqk", grad_block, value_heads, preferred_element_type=F32)
-        centre = jnp.sum(probs * prob_grad, axis=-1, keepdims=True)
-        score_grad = (probs * (prob_grad - centre)).astype(BF16)
-        query_grad = (
-            jnp.einsum("hqk,khd->qhd", score_grad, key_heads, preferred_element_type=F32) * scale
-        )
-        key_acc = (
-            key_acc
-            + jnp.einsum("hqk,qhd->khd", score_grad, query_block, preferred_element_type=F32)
-            * scale
-        )
-        return ((key_acc, value_acc), query_grad.astype(BF16))
-
-    empty = jnp.zeros((total_rows, head_count, HEAD), F32)
-    (key_total, value_total), query_grads = lax.scan(
-        back_block, (empty, empty), (query_blocks, mixed_blocks, log_totals)
-    )
-    return (
-        query_grads.reshape(total_rows, head_cols),
-        key_total.reshape(total_rows, head_cols).astype(BF16),
-        value_total.reshape(total_rows, head_cols).astype(BF16),
-    )
+CHUNK = 512
+SLOPE = math.log2(math.e) / math.sqrt(HEAD)
+SCALE = 1.0 / math.sqrt(HEAD)
+
+
+def lanes(rows):
+    return lax.broadcasted_iota(jnp.int32, (rows, 128), 1)
+
+
+def window(ref, slot, rows):
+    cols = ref[rows, pl.ds(slot // 2 * 128, 128)].astype(F32)
+    return cols if slot % 2 == 0 else pltpu.roll(cols, HEAD, 1)
+
+
+def pair_up(low, high):
+    return jnp.where(lanes(low.shape[0]) < HEAD, low, pltpu.roll(high, HEAD, 1))
+
+
+def chunk_at(k):
+    return pl.ds(pl.multiple_of(k * CHUNK, CHUNK), CHUNK)
+
+
+def head_at(h):
+    return pl.ds(pl.multiple_of(h * HEAD, HEAD), HEAD)
+
+
+def prepare_keys(length, packed, heads, queries, keys, rows):
+    lane = lanes(CHUNK)
+    start = rows * CHUNK + lax.broadcasted_iota(jnp.int32, (CHUNK, 128), 0)
+    bias = jnp.where(start < length, 0.0, NEGATIVE)
+    at = chunk_at(rows)
+    for h in range(heads):
+        query = window(packed, h, at)
+        queries[h, at] = jnp.where(lane < HEAD, query, jnp.where(lane == HEAD, 1.0, 0.0)).astype(BF16)
+        key = window(packed, heads + h, at)
+        keys[h, at] = jnp.where(lane < HEAD, key, jnp.where(lane == HEAD, bias, 0.0)).astype(BF16)
+
+
+def forward_kernel(heads, length, packed, mixed, logs, queries, keys, values_t, mixed_t):
+    chunks = packed.shape[0] // CHUNK
+
+    def prepare(k):
+        prepare_keys(length[0], packed, heads, queries, keys, k)
+        for h in range(heads):
+            value = window(packed, 2 * heads + h, chunk_at(k))
+            values_t[pl.ds(h * HEAD, HEAD), chunk_at(k)] = jnp.transpose(value)[:HEAD].astype(BF16)
+
+    loop(chunks, prepare)
+
+    def attend(step):
+        h, block = step // chunks, step % chunks
+        query = queries[h, chunk_at(block)]
+        top = jnp.full((1, CHUNK), -jnp.inf, F32)
+        total = jnp.zeros((1, CHUNK), F32)
+        mix = jnp.zeros((HEAD, CHUNK), F32)
+        for k in range(chunks):
+            scores = mm(keys[h, pl.ds(k * CHUNK, CHUNK)], query, ((1,), (1,)))
+            fresh = jnp.maximum(top, jnp.max(scores, axis=0, keepdims=True))
+            expo = jnp.exp2(scores * SLOPE - fresh * SLOPE)
+            keep = jnp.exp2((top - fresh) * SLOPE)
+            total = total * keep + jnp.sum(expo, axis=0, keepdims=True)
+            value = values_t[head_at(h), pl.ds(k * CHUNK, CHUNK)]
+            mix = mix * keep + mm(value, expo.astype(BF16), ((1,), (0,)))
+            top = fresh
+        mixed_t[head_at(h), chunk_at(block)] = mix / total
+        logs[h, :, chunk_at(block)] = jnp.broadcast_to(top * SLOPE + jnp.log2(total), (8, CHUNK))
+
+    loop(heads * chunks, attend)
+    spare = mixed_t.shape[0] - heads * HEAD
+    if spare:
+        mixed_t[pl.ds(heads * HEAD, spare)] = jnp.zeros((spare, mixed_t.shape[1]), F32)
+
+    def collect(k):
+        for pair in range(mixed_t.shape[0] // 128):
+            part = mixed_t[pl.ds(pair * 128, 128), chunk_at(k)]
+            mixed[chunk_at(k), pl.ds(pair * 128, 128)] = jnp.transpose(part).astype(BF16)
+
+    loop(chunks, collect)
+
+
+def attention_forward(packed, length, heads):
+    rows = packed.shape[0]
+    wide = -(-heads // 2) * 128
+    pieces = heads * rows * rows
+    return pl.pallas_call(
+        lambda *refs: forward_kernel(heads, *refs),
+        out_shape=(
+            jax.ShapeDtypeStruct((rows, wide), BF16),
+            jax.ShapeDtypeStruct((heads, 8, rows), F32),
+        ),
+        in_specs=[pl.BlockSpec(memory_space=pltpu.SMEM), vmem()],
+        out_specs=(vmem(), vmem()),
+        scratch_shapes=[
+            pltpu.VMEM((heads, rows, 128), BF16),
+            pltpu.VMEM((heads, rows, 128), BF16),
+            pltpu.VMEM((wide, rows), BF16),
+            pltpu.VMEM((wide, rows), F32),
+        ],
+        cost_estimate=pl.CostEstimate(
+            flops=4 * pieces * 256, bytes_accessed=80 << 20, transcendentals=pieces
+        ),
+        name="attention_forward",
+    )(length, packed)
+
+
+def backward_kernel(
+    heads, length, packed, mixed, grad, logs, out, sums, queries, keys, values, grads, keys_t, query_t,
+    key_acc, value_acc,
+):
+    chunks = packed.shape[0] // CHUNK
+    lane = lanes(CHUNK)
+
+    def prepare(k):
+        at = chunk_at(k)
+        prepare_keys(length[0], packed, heads, queries, keys, k)
+        for h in range(heads):
+            key = window(packed, heads + h, at)
+            keys_t[pl.ds(h * HEAD, HEAD), at] = jnp.transpose(key)[:HEAD].astype(BF16)
+            value = window(packed, 2 * heads + h, at)
+            ones = jnp.where(lane < HEAD + 3, 1.0, 0.0)
+            values[h, at] = jnp.where(lane < HEAD, value, ones).astype(BF16)
+            above = window(grad, h, at)
+            product = jnp.where(lane < HEAD, above * window(mixed, h, at), 0.0)
+            centre = jnp.sum(product, axis=1, keepdims=True)
+            first = centre.astype(BF16).astype(F32)
+            second = (centre - first).astype(BF16).astype(F32)
+            third = centre - first - second
+            extra = jnp.where(
+                lane == HEAD, first, jnp.where(lane == HEAD + 1, second, jnp.where(lane == HEAD + 2, third, 0.0))
+            )
+            grads[h, at] = jnp.where(lane < HEAD, above, -extra).astype(BF16)
+            key_acc[h, at] = jnp.zeros((CHUNK, 128), F32)
+            value_acc[h, at] = jnp.zeros((CHUNK, 128), F32)
+
+    loop(chunks, prepare)
+
+    def attend(step):
+        h, block = step // chunks, step % chunks
+        query = queries[h, chunk_at(block)]
+        above = grads[h, chunk_at(block)]
+        log = logs[h, pl.ds(0, 1), chunk_at(block)]
+        query_grad = jnp.zeros((HEAD, CHUNK), F32)
+        for k in range(chunks):
+            at = pl.ds(k * CHUNK, CHUNK)
+            scores = mm(keys[h, at], query, ((1,), (1,)))
+            probs = jnp.exp2(scores * SLOPE - log)
+            centred = mm(values[h, at], above, ((1,), (1,)))
+            score_grad = (probs * centred).astype(BF16)
+            value_acc[h, at] += mm(probs.astype(BF16), above, ((1,), (0,)))
+            key_acc[h, at] += mm(score_grad, query, ((1,), (0,)))
+            query_grad = query_grad + mm(keys_t[head_at(h), at], score_grad, ((1,), (0,)))
+        query_t[head_at(h), chunk_at(block)] = query_grad * SCALE
+
+    loop(heads * chunks, attend)
+    sums[...] = jnp.zeros_like(sums)
+    spare = query_t.shape[0] - heads * HEAD
+    if spare:
+        query_t[pl.ds(heads * HEAD, spare)] = jnp.zeros((spare, query_t.shape[1]), F32)
+
+    def collect(k):
+        at = chunk_at(k)
+
+        def slot(index):
+            h = index % heads
+            if index < heads:
+                rows = jnp.transpose(query_t[pl.ds(h // 2 * 128, 128), at])
+                return rows if h % 2 == 0 else pltpu.roll(rows, HEAD, 1)
+            if index < 2 * heads:
+                return key_acc[h, at] * SCALE
+            if index < 3 * heads:
+                return value_acc[h, at]
+            return jnp.zeros((CHUNK, 128), F32)
+
+        for pair in range(out.shape[1] // 128):
+            part = pair_up(slot(2 * pair), slot(2 * pair + 1)).astype(BF16)
+            out[at, pl.ds(pair * 128, 128)] = part
+            sums[:, pl.ds(pair * 128, 128)] += jnp.sum(part.astype(F32), axis=0, keepdims=True)
+
+    loop(chunks, collect)
+
+
+def attention_backward(packed, mixed, grad, logs, length, heads):
+    rows, width = packed.shape
+    wide = -(-heads // 2) * 128
+    pieces = heads * rows * rows
+    return pl.pallas_call(
+        lambda *refs: backward_kernel(heads, *refs),
+        out_shape=(
+            jax.ShapeDtypeStruct((rows, width), BF16),
+            jax.ShapeDtypeStruct((8, width), F32),
+        ),
+        in_specs=[pl.BlockSpec(memory_space=pltpu.SMEM)] + [vmem()] * 4,
+        out_specs=(vmem(), vmem()),
+        scratch_shapes=[pltpu.VMEM((heads, rows, 128), BF16)] * 4
+        + [pltpu.VMEM((wide, rows), BF16), pltpu.VMEM((wide, rows), F32)]
+        + [pltpu.VMEM((heads, rows, 128), F32)] * 2,
+        cost_estimate=pl.CostEstimate(
+            flops=10 * pieces * 256, bytes_accessed=200 << 20, transcendentals=pieces
+        ),
+        name="attention_backward",
+    )(length, packed, mixed, grad, logs)
 
 
 def per_device(
@@ -483,9 +612,15 @@
     unit_cols = up_weight.shape[1]
     depth = up_weight.shape[0]
     length = lengths[0]
-    qkv_rows = jnp.concatenate([qkv_weight[0], qkv_weight[1], qkv_weight[2]], axis=1)
+    heads = head_cols // HEAD
+    pad_qkv = -(-3 * heads // 2) * 128 - 3 * head_cols
+    pad_out = -(-heads // 2) * 128 - head_cols
+    qkv_rows = jnp.pad(
+        jnp.concatenate([qkv_weight[0], qkv_weight[1], qkv_weight[2]], axis=1), ((0, 0), (0, pad_qkv))
+    )
     seq_tokens, qkv_full = start_gather(tokens, qkv_rows)
-    rest_rows = jnp.concatenate([up_weight, down_weight.T, out_weight.T], axis=1)
+    out_rows = jnp.pad(out_weight.T, ((0, 0), (0, pad_out)))
+    rest_rows = jnp.concatenate([up_weight, down_weight.T, out_rows], axis=1)
     rest_full = lax.all_gather(rest_rows, "dp", axis=0, tiled=True)
     up_full = rest_full[:, :unit_cols]
     down_full = rest_full[:, unit_cols : 2 * unit_cols]
@@ -495,12 +630,11 @@
     head_start = piece * head_cols
     unit_start = piece * unit_cols
     bias_cols = lax.dynamic_slice_in_dim(qv_bias, head_start, head_cols, 1)
-    qkv_bias = jnp.concatenate([bias_cols[0], jnp.zeros((head_cols,), F32), bias_cols[1]])
+    qkv_bias = jnp.concatenate(
+        [bias_cols[0], jnp.zeros((head_cols,), F32), bias_cols[1], jnp.zeros((pad_qkv,), F32)]
+    )
     projected = (mm(seq_tokens, qkv_full, ((1,), (0,))) + qkv_bias).astype(BF16)
-    queries = projected[:, :head_cols]
-    key_rows = projected[:, head_cols : 2 * head_cols]
-    value_rows = projected[:, 2 * head_cols :]
-    mixed, log_totals = attention_forward(queries, key_rows, value_rows, length)
+    mixed, logs = attention_forward(projected, lengths, heads)
     attn_local = scatter_tensor(mixed, out_full, 2)
     first_out, first_normed, first_inverse = norm_rows(
         tokens.astype(F32) + (attn_local + out_bias), first_gain, first_shift
@@ -538,17 +672,14 @@
     seq_attn_grad = gather_tensor(attn_grad, 7)
     out_grad = mm(seq_attn_grad, mixed, ((0,), (0,))).astype(BF16)
     mixed_grad = mm(seq_attn_grad, out_full, ((1,), (0,))).astype(BF16)
-    query_grad, key_grad, value_grad = attention_backward(
-        queries, key_rows, value_rows, mixed_grad, log_totals, length
-    )
-    stacked = jnp.concatenate([query_grad, key_grad, value_grad], axis=1)
+    stacked, sums = attention_backward(projected, mixed, mixed_grad, logs, lengths, heads)
     qkv_grad = mm(seq_tokens, stacked, ((0,), (0,))).astype(BF16)
     zeros_heads = jnp.zeros((width,), F32)
     query_bias = lax.dynamic_update_slice(
-        zeros_heads, jnp.sum(query_grad.astype(F32), axis=0), (head_start,)
+        zeros_heads, sums[0, :head_cols], (head_start,)
     )
     value_bias = lax.dynamic_update_slice(
-        zeros_heads, jnp.sum(value_grad.astype(F32), axis=0), (head_start,)
+        zeros_heads, sums[0, 2 * head_cols : 3 * head_cols], (head_start,)
     )
     up_bias_full = lax.dynamic_update_slice(
         jnp.zeros((up_bias.shape[0],), F32), up_bias_part, (unit_start,)
@@ -573,7 +704,8 @@
     bits_wide = small.shape[1]
     padded = -(-bits_wide // 1024) * 1024
     small = jnp.pad(small, ((0, 0), (0, padded - bits_wide))).reshape(ways, -1, 128)
-    grads = jnp.concatenate([qkv_grad, out_grad], axis=1).reshape(-1, depth, 4 * head_cols)
+    grads = jnp.concatenate([qkv_grad, out_grad], axis=1)
+    grads = grads.reshape(-1, depth, grads.shape[1])
     token_back, grad_qo, small = tail(stacked, qkv_full, grads, small)
     small = small.reshape(-1)
     grad_tokens = grad_first + token_back
@@ -589,7 +721,7 @@
         grad_tokens,
         grad_qkv,
         jnp.stack([bits[0], bits[1]]),
-        grad_qo[:, 3 * head_cols :].T,
+        grad_qo[:, 3 * head_cols + pad_qkv :][:, :head_cols].T,
         bits[2],
         bits[3],
         bits[4],

time: 524 us -> 410 us (0.78)
  matrix products: 149 us -> 42.5 us
  Pallas kernels: 239 us -> 309 us
  other arithmetic: 70.7 us -> 22.3 us
  local copies, waits for them, and re-layouts: 44 us -> 20.5 us
    dot_general x28 -> x0, matrix products: 107 us -> none  [the longest x4 22.7 us: back_block(): jnp.einsum('hqk,khd->qhd', score_grad, key_heads, preferred_element_type=...]
    pallas_call x0 -> x2, Pallas kernels: none -> 76.3 us  [the longest x1 43.9 us: attention_backward(): pl.pallas_call(lambda *refs: backward_kernel(heads, *refs), out_shape=(ja...]
    convert_element_type x5 -> x0, other arithmetic: 20 us -> none  [the longest x4 19.9 us: back_block(): score_grad = (probs * (prob_grad - centre)).astype(BF16)]
    reduce_sum x6 -> x0, other arithmetic: 13.9 us -> none  [the longest x4 11.2 us: attend_block(): row_total = jnp.sum(expo, axis=-1, keepdims=True)]
    pallas_call x3, Pallas kernels: 88.5 us -> 77.2 us  [scatter_tensor(): pl.pallas_call(scatter_kernel, out_shape=jax.ShapeDtypeStruct((rows, widt...]
    convert_element_type x4 -> x0, local copies, waits for them, and re-layouts: 6.72 us -> none  [the longest x2 4.65 us: attention_backward(): value_total.reshape(total_rows, head_cols).astype(BF16)]
  transfers between devices with their start and end apart: 2 -> 2, of which waited for: 0 -> 0; matrix products, arithmetic and copies ran while one was open for 37% -> 8% of each run, Pallas kernels for 16% -> 45%
where the time goes in v3:
time: 410 us; the launch traced here: 409 us
  Pallas kernels  309 us (75%)
  matrix products  42.5 us (10%)
  other arithmetic  22.3 us (5%)
  local copies, waits for them, and re-layouts  20.5 us (5%)
  between operations  15.1 us (4%)
    pallas_call x3, Pallas kernels, scatter_tensor(): pl.pallas_call(scatter_kernel, out_shape=jax.ShapeDtypeStruct((rows, widt...  77.2 us
    pallas_call x3, Pallas kernels, gather_tensor(): pl.pallas_call(gather_kernel, out_shape=jax.ShapeDtypeStruct((PARTS, coun...  70.4 us
    pallas_call x1, Pallas kernels, tail(): pl.pallas_call(tail_kernel, out_shape=(jax.ShapeDtypeStruct((rows, width)...  48.5 us
    pallas_call x1, Pallas kernels, attention_backward(): pl.pallas_call(lambda *refs: backward_kernel(heads, *refs), out_shape=(ja...  43.9 us
    dot_general x8, matrix products, mm(): lax.dot_general(left, right, (dims, ((), ())), preferred_element_type=F32)  42.5 us
    pallas_call x1, Pallas kernels, start_gather(): pl.pallas_call(start_kernel, out_shape=(jax.ShapeDtypeStruct((PARTS, coun...  36.2 us
    pallas_call x1, Pallas kernels, attention_forward(): pl.pallas_call(lambda *refs: forward_kernel(heads, *refs), out_shape=(jax...  32.4 us
  transfers between devices with their start and end apart: 2, of which 0 were waited for; matrix products, arithmetic and copies ran while one was open for 8% of the time, Pallas kernels for 45%

profile of v3, /device:TPU:0, one launch (start us, length us, event | category | flops | bytes accessed | tf_op | source)
XLA Modules:
  0.0 409.1 jit_solution(13637613664031663575)
XLA Ops:
  8.1 1.7 fusion.13
  12.2 36.2 %start_gather.1 = (bf16[4,512,768]{2,1,0:T(8,128)(2,1)}, bf16[8,96,640]{2,1,0:T(8,128)(2,1)}) custom-call(bf16[512,768]{1,0:T(8,128)(2,1)} %tokens.1, bf16[96,640]{1,0:T(8,128)(2,1)} %fusion.18.weight), custom_call_target="tpu_custom_call" | custom-call | bytes 62914560 | tf_op jit(solution)/shard_map/start_gather/pallas_call | solution.py:201
  50.2 6.3 %add_convert_fusion.refs_1_ = bf16[2048,640]{1,0:T(8,128)(2,1)} fusion(bf16[2048,768]{1,0:T(8,128)(2,1)} %bitcast.72, bf16[768,640]{1,0:T(8,128)(2,1)} %bitcast.74, f32[640]{0:T(1024)S(1)} %pad_maximum_fusion.3), kind=kOutput, calls=%fused_computation.13 | convolution fusion | flops 2015887360 | bytes 6752768 | tf_op jit(solution)/shard_map/dot_general | solution.py:40
  56.4 32.4 %attention_forward.1 = (bf16[2048,256]{1,0:T(8,128)(2,1)}, f32[3,8,2048]{2,1,0:T(8,128)}) custom-call(s32[1]{0:T(128)} %copy.39.refs_0_, bf16[2048,640]{1,0:T(8,128)(2,1)} %add_convert_fusion.refs_1_), custom_call_target="tpu_custom_call" | custom-call | flops 12884901888 | bytes 83886080 | tf_op jit(solution)/shard_map/attention_forward/pallas_call | solution.py:472
  88.9 1.8 slice.102.weight
  90.6 24.6 %scatter_rows_2.1 = f32[512,768]{1,0:T(8,128)} custom-call(bf16[4,512,256]{2,1,0:T(8,128)(2,1)} %bitcast.62, bf16[768,256]{1,0:T(8,128)(2,1)} %slice.102.weight), custom_call_target="tpu_custom_call" | custom-call | flops 805306368 | bytes 62914560 | tf_op jit(solution)/shard_map/scatter_rows_2/pallas_call | solution.py:303
  118.8 23.9 %gather_rows_3.1 = bf16[4,512,768]{2,1,0:T(8,128)(2,1)} custom-call(bf16[512,768]{1,0:T(8,128)(2,1)} %fusion.11.mine), custom_call_target="tpu_custom_call" | custom-call | bytes 62914560 | tf_op jit(solution)/shard_map/gather_rows_3/pallas_call | solution.py:154
  142.7 3.3 fusion.33
  146.1 7.1 %fusion.7 = (bf16[2048,768]{1,0:T(8,128)(2,1)}, f32[2048,768]{1,0:T(8,128)}) fusion(f32[768]{0:T(1024)S(1)} %dynamic_slice.7, bf16[2048,768]{1,0:T(8,128)(2,1)S(1)} %bitcast.57, bf16[768,1792]{1,0:T(8,128)(2,1)} %all-gather.2.cloned.1.call-done), kind=kOutput, calls=%fused_computation.12 | convolution fusion | flops 2431647744 | bytes 13765632 | tf_op jit(solution)/shard_map/dot_general | solution.py:40
  153.2 26.3 %scatter_rows_4.1 = f32[512,768]{1,0:T(8,128)} custom-call(bf16[4,512,768]{2,1,0:T(8,128)(2,1)} %bitcast.76, bf16[768,768]{1,0:T(8,128)(2,1)} %get-tuple-element.85.weight), custom_call_target="tpu_custom_call" | custom-call | flops 2415919104 | bytes 62914560 | tf_op jit(solution)/shard_map/scatter_rows_4/pallas_call | solution.py:303
  179.4 2.0 fusion.31
  184.9 23.4 %gather_rows_5.1 = bf16[4,512,768]{2,1,0:T(8,128)(2,1)} custom-call(bf16[512,768]{1,0:T(8,128)(2,1)} %get-tuple-element.75.mine), custom_call_target="tpu_custom_call" | custom-call | bytes 62914560 | tf_op jit(solution)/shard_map/gather_rows_5/pallas_call | solution.py:154
  208.4 6.7 %convolution_convert_fusion.1 = bf16[768,768]{1,0:T(8,128)(2,1)} fusion(bf16[2048,768]{1,0:T(8,128)(2,1)} %bitcast.59, bf16[2048,768]{1,0:T(8,128)(2,1)} %get-tuple-element.106), kind=kOutput, calls=%fused_computation.34 | convolution fusion | flops 2416508928 | bytes 7471104 | tf_op jit(solution)/shard_map/dot_general | solution.py:40
  215.1 9.3 %convert_reduce_fusion = (f32[768]{0:T(1024)S(1)}, bf16[2048,768]{1,0:T(8,128)(2,1)S(1)}) fusion(f32[2048,768]{1,0:T(8,128)} %get-tuple-element.107, f32[768]{0:T(1024)S(1)} %dynamic_slice.7, bf16[2048,768]{1,0:T(8,128)(2,1)S(1)} %bitcast.60, bf16[768,1792]{1,0:T(8,128)(2,1)} %all-gather.2.cloned.1.call-done), kind=kOutput, calls=%fused_computation.10 | convolution fusion | flops 2458385664 | bytes 13768704 | tf_op jit(solution)/shard_map/dot_general | solution.py:40
  224.4 3.7 convolution_convert_fusion.2
  228.2 26.3 %scatter_rows_6.1 = f32[512,768]{1,0:T(8,128)} custom-call(bf16[4,512,768]{2,1,0:T(8,128)(2,1)} %bitcast.77, bf16[768,768]{1,0:T(8,128)(2,1)} %get-tuple-element.84.weight), custom_call_target="tpu_custom_call" | custom-call | flops 2415919104 | bytes 62914560 | tf_op jit(solution)/shard_map/scatter_rows_6/pallas_call | solution.py:303
  254.5 3.8 multiply_reduce_fusion.1
  261.8 23.1 %gather_rows_7.1 = bf16[4,512,768]{2,1,0:T(8,128)(2,1)} custom-call(bf16[512,768]{1,0:T(8,128)(2,1)} %get-tuple-element.29.mine), custom_call_target="tpu_custom_call" | custom-call | bytes 62914560 | tf_op jit(solution)/shard_map/gather_rows_7/pallas_call | solution.py:154
  284.8 3.9 convolution_convert_fusion.refs_3_
  288.8 43.9 %attention_backward.1 = (bf16[2048,640]{1,0:T(8,128)(2,1)}, f32[8,640]{1,0:T(8,128)}) custom-call(s32[1]{0:T(128)} %copy.39.refs_0_, bf16[2048,640]{1,0:T(8,128)(2,1)} %add_convert_fusion.refs_1_, bf16[2048,256]{1,0:T(8,128)(2,1)} %get-tuple-element.28.refs_2_, bf16[2048,256]{1,0:T(8,128)(2,1)} %convolution_convert_fusion.refs_3_, ...), custom_call_target="tpu_custom_call" | custom-call | flops 32212254720 | bytes 209715200 | tf_op jit(solution)/shard_map/attention_backward/pallas_call | solution.py:573
  335.7 3.1 convolution_convert_fusion.4
  339.3 2.4 convolution_convert_fusion.3
  343.4 48.5 %tail.1 = (f32[512,768]{1,0:T(8,128)}, f32[96,896]{1,0:T(8,128)}, f32[8,128]{1,0:T(8,128)}) custom-call(bf16[4,512,640]{2,1,0:T(8,128)(2,1)} %bitcast.78, bf16[768,640]{1,0:T(8,128)(2,1)} %bitcast.75, bf16[8,96,896]{2,1,0:T(8,128)(2,1)} %bitcast.61, f32[32,8,128]{2,1,0:T(8,128)} %bitcast.65), custom_call_target="tpu_custom_call" | custom-call | flops 2013265920 | bytes 94371840 | tf_op jit(solution)/shard_map/tail/pallas_call | solution.py:364
  395.1 2.7 add.135
  (98 shorter events, 27.6 us)
Async XLA Ops:
  7.2 81.7 %all-gather.2.cloned.1.call-start = ((), (), s32[]{:S(2)}) async-start(), calls=%async_computation.1 | async-start | bytes 3096576 | tf_op jit(solution)/shard_map/all_gather | solution.py:624
  9.9 389.8 %reduce-scatter.2.cloned.1.call-start = ((), (), s32[]{:S(2)}) async-start(), calls=%async_computation.2 | async-start | bytes 2654208 | tf_op jit(solution)/shard_map/reduce_scatter | solution.py:669
  90.6 24.6 %copy-start.1 = (bf16[512,768]{1,0:T(8,128)(2,1)S(1)}, bf16[512,768]{1,0:T(8,128)(2,1)}, u32[]{:S(2)}) copy-start(bf16[512,768]{1,0:T(8,128)(2,1)} %tokens.1) | copy-start | bytes 2359300
  90.6 24.6 %copy-start.14 = (f32[768]{0:T(1024)S(1)}, f32[768]{0:T(1024)}, u32[]{:S(2)}) copy-start(f32[768]{0:T(1024)} %param.20) | copy-start | bytes 9220
  116.9 0.7 copy-start.9
  117.0 0.7 copy-start.11
  142.7 3.4 copy-start.2
  153.1 26.3 %copy-start.15 = (f32[768]{0:T(1024)S(1)}, f32[768]{0:T(1024)}, u32[]{:S(2)}) copy-start(f32[768]{0:T(1024)} %param.26) | copy-start | bytes 9220
  181.4 1.1 copy-start
  181.4 1.1 copy-start.10
  208.4 6.7 %copy-start.4 = (bf16[4,512,768]{2,1,0:T(8,128)(2,1)S(1)}, bf16[4,512,768]{2,1,0:T(8,128)(2,1)}, u32[]{:S(2)}) copy-start(bf16[4,512,768]{2,1,0:T(8,128)(2,1)} %gather_rows_5.1) | copy-start | bytes 9437188
  215.1 9.3 %copy-start.3 = (bf16[4,512,768]{2,1,0:T(8,128)(2,1)S(1)}, bf16[4,512,768]{2,1,0:T(8,128)(2,1)}, u32[]{:S(2)}) copy-start(bf16[4,512,768]{2,1,0:T(8,128)(2,1)} %gather_rows_3.1) | copy-start | bytes 9437188
  224.4 3.7 copy-start.17
  228.2 26.3 %copy-start.12 = (f32[768]{0:T(1024)S(1)}, f32[768]{0:T(1024)}, u32[]{:S(2)}) copy-start(f32[768]{0:T(1024)} %param.28) | copy-start | bytes 9220
  258.2 1.4 copy-start.6
  258.3 1.9 copy-start.7
  288.8 46.9 %copy-start.8 = (bf16[2048,256]{1,0:T(8,128)(2,1)S(1)}, bf16[2048,256]{1,0:T(8,128)(2,1)}, u32[]{:S(2)}) copy-start(bf16[2048,256]{1,0:T(8,128)(2,1)} %get-tuple-element.28.refs_2_) | copy-start | bytes 3145732
  335.7 3.1 copy-start.16
  335.7 3.7 copy-start.18
  395.1 2.7 copy-start.13
  399.7 1.8 copy-start.5
Sparse Core Ops, SparseCore 0:
  10.7 73.4 all-gather.1
  261.9 75.1 reduce-scatter.1
